TPU v7x, 8 devices: a whole 2x2x1 slice. The times are simulated.
8 devices in a mesh: t: 4 (over z, y, x), v: 2 (over core).
Axes of the slice: x: 2, y: 2, z: 1, core: 2. Of those that a mesh axis runs over, the one named last changes fastest.
Arguments:
- hidden_in: bfloat16 [1024, 2304], replicated
- seq_lens: int32 [1024], replicated
- target: int32 [1024], replicated
- g_attn_pre: bfloat16 [2304], replicated
- w_q: bfloat16 [2304, 2048], P(None, 't')
- w_k: bfloat16 [2304, 1024], P(None, 't')
- w_v: bfloat16 [2304, 1024], P(None, 't')
- w_o: bfloat16 [2048, 2304], P('t')
- g_attn_post: bfloat16 [2304], replicated
- g_mlp_pre: bfloat16 [2304], replicated
- w_gate: bfloat16 [2304, 9216], P(None, 't')
- w_up: bfloat16 [2304, 9216], P(None, 't')
- w_down: bfloat16 [9216, 2304], P('t')
- g_mlp_post: bfloat16 [2304], replicated
- g_final: bfloat16 [2304], replicated
- k_cache: bfloat16 [1024, 32, 4, 256], P(None, None, 't')
- v_cache: bfloat16 [1024, 32, 4, 256], P(None, None, 't')
- embed_table: bfloat16 [256000, 2304], P(('v', 't'))
Outputs:
- output 1: float32 [1024], replicated
- output 2: bfloat16 [1024, 2304], replicated
All inputs are finite; a program needn't handle non-finite values.
Results may differ from a plain program's by a relative error of at most 0.00791178.
Values sent between devices are 32-bit elements.
A program may use at most 1 GiB of HBM per device.

v0:
```python
import jax
import jax.numpy as jnp
from jax import lax
from jax.sharding import PartitionSpec as P

ATTN_CAP = 50.0
FINAL_CAP = 30.0
NORM_EPS = 1e-6
ROPE_BASE = 10000.0


def rms_norm(values, gain_vec):
    x_f32 = values.astype(jnp.float32)
    scaled = x_f32 * lax.rsqrt(jnp.mean(x_f32 * x_f32, axis=-1, keepdims=True) + NORM_EPS)
    return scaled * (1.0 + gain_vec.astype(jnp.float32))


def rotary(values, positions):
    half_dim = values.shape[-1] // 2
    inv_freq = ROPE_BASE ** (-2.0 * jnp.arange(half_dim, dtype=jnp.float32) / values.shape[-1])
    angles = positions.astype(jnp.float32)[:, None] * inv_freq[None, :]
    angles = angles.reshape((values.shape[0],) + (1,) * (values.ndim - 2) + (half_dim,))
    cos_t = jnp.cos(angles)
    sin_t = jnp.sin(angles)
    x_low = values[..., :half_dim]
    x_high = values[..., half_dim:]
    return jnp.concatenate([x_low * cos_t - x_high * sin_t, x_high * cos_t + x_low * sin_t], axis=-1)


def attention(normed, seq_lens, w_q, w_k, w_v, k_cache, v_cache):
    tokens, ctx_len, kv_heads, head_dim = k_cache.shape
    group_size = w_q.shape[1] // (kv_heads * head_dim)
    score_scale = head_dim ** -0.5
    q_rot = rotary(jnp.dot(normed, w_q, preferred_element_type=jnp.float32).reshape(tokens, kv_heads, group_size, head_dim), seq_lens).astype(jnp.bfloat16)
    k_rot = rotary(jnp.dot(normed, w_k, preferred_element_type=jnp.float32).reshape(tokens, kv_heads, head_dim), seq_lens).astype(jnp.bfloat16)
    v_new = jnp.dot(normed, w_v, preferred_element_type=jnp.float32).astype(jnp.bfloat16).reshape(tokens, kv_heads, head_dim)
    s_cache = jnp.einsum('nkgd,ntkd->nkgt', q_rot, k_cache, preferred_element_type=jnp.float32) * score_scale
    s_new = jnp.einsum('nkgd,nkd->nkg', q_rot, k_rot, preferred_element_type=jnp.float32) * score_scale
    s_cache = ATTN_CAP * jnp.tanh(s_cache / ATTN_CAP)
    s_new = ATTN_CAP * jnp.tanh(s_new / ATTN_CAP)
    valid_mask = jnp.arange(ctx_len)[None, :] < seq_lens[:, None]
    s_cache = jnp.where(valid_mask[:, None, None, :], s_cache, -1e30)
    row_max = jnp.maximum(jnp.max(s_cache, axis=-1), s_new)
    p_cache = jnp.exp(s_cache - row_max[..., None])
    p_new = jnp.exp(s_new - row_max)
    denominator = jnp.sum(p_cache, axis=-1) + p_new
    weighted = jnp.einsum('nkgt,ntkd->nkgd', p_cache.astype(jnp.bfloat16), v_cache, preferred_element_type=jnp.float32)
    weighted = weighted + p_new.astype(jnp.bfloat16).astype(jnp.float32)[..., None] * v_new.astype(jnp.float32)[:, :, None, :]
    return (weighted / denominator[..., None]).astype(jnp.bfloat16).reshape(tokens, kv_heads * group_size * head_dim)


def solution(mesh):
    tp_size = mesh.shape['t']
    in_specs = (P(), P(), P(), P(), P(None, 't'), P(None, 't'), P(None, 't'), P('t', None), P(), P(), P(None, 't'), P(None, 't'), P('t', None), P(), P(), P(None, None, 't', None), P(None, None, 't', None), P(('v', 't'), None))

    def local_step(hidden_in, seq_lens, target, g_attn_pre, w_q, w_k, w_v, w_o, g_attn_post, g_mlp_pre, w_gate, w_up, w_down, g_mlp_post, g_final, k_cache, v_cache, embed_table):
        normed = rms_norm(hidden_in, g_attn_pre).astype(jnp.bfloat16)
        attn_vec = attention(normed, seq_lens, w_q, w_k, w_v, k_cache, v_cache)
        attn_part = jnp.dot(attn_vec, w_o, preferred_element_type=jnp.float32)
        attn_out = lax.psum(attn_part, 't')
        hidden_mid = (hidden_in.astype(jnp.float32) + rms_norm(attn_out, g_attn_post)).astype(jnp.bfloat16)
        mlp_in = rms_norm(hidden_mid, g_mlp_pre).astype(jnp.bfloat16)
        gate_proj = jnp.dot(mlp_in, w_gate, preferred_element_type=jnp.float32)
        up_proj = jnp.dot(mlp_in, w_up, preferred_element_type=jnp.float32)
        activated = (jax.nn.gelu(gate_proj, approximate=True) * up_proj).astype(jnp.bfloat16)
        mlp_part = jnp.dot(activated, w_down, preferred_element_type=jnp.float32)
        mlp_out = lax.psum(mlp_part, 't')
        hidden_out = (hidden_mid.astype(jnp.float32) + rms_norm(mlp_out, g_mlp_post)).astype(jnp.bfloat16)
        final_h = rms_norm(hidden_out, g_final).astype(jnp.bfloat16)
        logits = lax.dot_general(final_h, embed_table, (((1,), (1,)), ((), ())), preferred_element_type=jnp.float32)
        capped = FINAL_CAP * jnp.tanh(logits / FINAL_CAP)
        vocab_local = embed_table.shape[0]
        shard_index = lax.axis_index('v') * tp_size + lax.axis_index('t')
        row_ids = shard_index * vocab_local + jnp.arange(vocab_local)
        local_max = jnp.max(capped, axis=1)
        local_sum = jnp.sum(jnp.exp(capped - local_max[:, None]), axis=1)
        local_tgt = jnp.sum(jnp.where(row_ids[None, :] == target[:, None], capped, 0.0), axis=1)
        gathered = lax.all_gather(jnp.stack([local_max, local_sum, local_tgt]), ('v', 't'))
        glob_max = jnp.max(gathered[:, 0], axis=0)
        glob_sum = jnp.sum(gathered[:, 1] * jnp.exp(gathered[:, 0] - glob_max[None, :]), axis=0)
        logprob = jnp.sum(gathered[:, 2], axis=0) - glob_max - jnp.log(glob_sum)
        return logprob, hidden_out

    return jax.shard_map(local_step, mesh=mesh, in_specs=in_specs, out_specs=(P(), P()), check_vma=False)
```

profile of v0, /device:TPU:0, one launch (start us, length us, event | category | flops | bytes accessed | tf_op | source)
XLA Modules:
  0.0 769.4 jit_solution(16212316745833335456)
XLA Ops:
  10.2 3.3 fusion.8
  13.5 5.7 fusion.80
  20.3 2.3 copy.46
  23.9 4.3 convolution_bitcast_fusion
  28.3 3.1 multiply_cosine_fusion.1
  31.4 2.3 fusion.68
  36.3 2.5 fusion.65
  39.8 3.1 multiply_reduce_fusion.2
  44.1 9.2 %fusion.85 = (f32[1024,2]{1,0:T(8,128)S(1)}, f32[1024,2,32]{2,1,0:T(2,128)}) fusion(bf16[1024,32,1,256]{3,1,2,0:T(8,128)(2,1)} %param.33, bf16[1024,2,128]{2,1,0:T(2,128)(2,1)} %copy-done.4, bf16[1024,2,128]{2,1,0:T(2,128)(2,1)} %copy-done.3, pred[1024,32]{1,0:T(8,128)(4,1)S(1)} %iota_compare_fusion), kind=kOutput, calls=%fused_computation.115 | convolution fusion | flops 35911680 | bytes 18128896 | tf_op jit(solution)/shard_map/nkgd,ntkd->nkgt/dot_general | solution.py:37
  53.8 15.5 %fusion.57 = f32[1024,2]{1,0:T(8,128)S(1)} fusion(f32[1024,2,32]{2,1,0:T(2,128)} %get-tuple-element.23, f32[1024,2]{1,0:T(8,128)S(1)} %copy.35), kind=kLoop, calls=%fused_computation.70 | loop fusion | flops 129024 | bytes 278528 | tf_op jit(solution)/shard_map/reduce_sum | solution.py:46
  70.8 4.3 fusion.39
  75.1 8.2 %fusion.34 = bf16[1024,2,256]{2,1,0:T(2,128)(2,1)S(1)} fusion(bf16[1024,32,1,256]{3,1,2,0:T(8,128)(2,1)} %param.34, f32[1024,2]{1,0:T(8,128)S(1)} %copy-done.7, f32[1024,256]{1,0:T(8,128)S(1)} %fusion.39, f32[1024,2]{1,0:T(8,128)S(1)} %copy.36, f32[1024,2,32]{2,1,0:T(2,128)S(1)} %copy-done.5, f32[1024,2]{1,0:T(8,128)S(1)} %copy.35), kind=kOutput, calls=%fused_computation.49 | convolution fusion | flops 35782656 | bytes 19161088 | tf_op jit(solution)/shard_map/nkgt,ntkd->nkgd/dot_general | solution.py:47
  83.5 5.1 fusion.86
  88.7 179.7 %all-reduce.3.cloned.1.call-done = f32[1024,2304]{1,0:T(8,128)} async-done(((f32[1024,2304]{1,0:T(8,128)}), f32[1024,2304]{1,0:T(8,128)}) %all-reduce.3.cloned.1.call-update) | async-done | bytes 9437200 | tf_op jit(solution)/shard_map/psum | solution.py:60
  268.4 4.4 multiply_reduce_fusion.1
  272.8 6.3 fusion.12
  281.3 15.7 %fusion.37 = f32[1024,2304]{1,0:T(8,128)} fusion(bf16[2304,2304]{1,0:T(8,128)(2,1)} %param.28, bf16[1024,2304]{1,0:T(8,128)(2,1)S(1)} %get-tuple-element.9, f32[2304]{0:T(1024)S(1)} %convert_add_fusion.4, f32[1024]{0:T(1024)S(1)} %add_rsqrt_fusion.2), kind=kOutput, calls=%fused_computation.51 | convolution fusion | flops 10881073152 | bytes 24785920 | tf_op jit(solution)/shard_map/dot_general | solution.py:63
  297.0 35.0 %fusion.25 = f32[1024,2304]{1,0:T(8,128)} fusion(bf16[2304,2304]{1,0:T(8,128)(2,1)} %param.30, f32[1024,2304]{1,0:T(8,128)} %fusion.37, bf16[2304,2304]{1,0:T(8,128)(2,1)} %param.29, bf16[1024,2304]{1,0:T(8,128)(2,1)} %copy-done.2, f32[2304]{0:T(1024)S(1)} %convert_add_fusion.4, f32[1024]{0:T(1024)S(1)} %add_rsqrt_fusion.2), kind=kOutput, calls=%fused_computation.39 | convolution fusion | flops 21776302080 | bytes 44839936 | tf_op jit(solution)/shard_map/dot_general | solution.py:66
  333.4 175.6 %all-reduce.5.cloned.1.call-done = f32[1024,2304]{1,0:T(8,128)} async-done(((f32[1024,2304]{1,0:T(8,128)}), f32[1024,2304]{1,0:T(8,128)}) %all-reduce.5.cloned.1.call-update) | async-done | bytes 9437200 | tf_op jit(solution)/shard_map/psum | solution.py:67
  509.0 4.4 multiply_reduce_fusion
  513.3 9.3 %fusion.5 = (f32[1024]{0:T(1024)S(1)}, bf16[1024,2304]{1,0:T(8,128)(2,1)}) fusion(f32[2304]{0:T(1024)S(1)} %convert_add_fusion.3, f32[1024,2304]{1,0:T(8,128)} %all-reduce.5.cloned.1.call-done, f32[1024]{0:T(1024)S(1)} %add_rsqrt_fusion.1, bf16[1024,2304]{1,0:T(8,128)(2,1)} %copy-done.2), kind=kLoop, calls=%fused_computation.17 | loop fusion | flops 18873344 | bytes 18891776 | tf_op jit(solution)/shard_map/reduce_sum | solution.py:14
  522.6 168.3 %fusion = (f32[1024]{0:T(1024)S(1)}, f32[1024,32000]{1,0:T(8,128)}) fusion(bf16[32000,2304]{1,0:T(8,128)(2,1)} %param.35, bf16[1024,2304]{1,0:T(8,128)(2,1)} %get-tuple-element.7, f32[2304]{0:T(1024)S(1)} %convert_add_fusion.2, f32[1024]{0:T(1024)S(1)} %add_rsqrt_fusion), kind=kOutput, calls=%fused_computation.3 | convolution fusion | flops 151102685184 | bytes 283264000 | tf_op jit(solution)/shard_map/dot_general | solution.py:70
  691.0 59.2 %exponential_reduce_fusion = (f32[1024]{0:T(1024)S(1)}, f32[1024]{0:T(1024)S(1)}) fusion(f32[1024,32000]{1,0:T(8,128)} %get-tuple-element.25, f32[1024]{0:T(1024)S(1)} %get-tuple-element.24, s32[1024]{0:T(1024)S(1)} %copy-done.13, s32[32000]{0:T(1024)S(1)} %copy-done.6), kind=kLoop, calls=%fused_computation.1 | loop fusion | flops 229373952 | bytes 131216384 | tf_op jit(solution)/shard_map/reduce_sum | solution.py:76
  750.2 11.1 %all-gather.1 = f32[8,3,1024]{2,1,0:T(4,128)S(1)} all-gather(f32[1,3,1024]{2,1,0:T(4,128)S(1)} %maximum_bitcast_fusion), channel_id=2, replica_groups=mesh['t'=4,'v'=2] {'v','t'}, dimensions={0}, use_global_device_ids=true | all-gather | bytes 110592 | tf_op jit(solution)/shard_map/all_gather | solution.py:78
  (69 shorter events, 16.8 us)
Async XLA Ops:
  7.2 76.4 %copy-start = (bf16[512,2304]{1,0:T(8,128)(2,1)S(1)}, bf16[512,2304]{1,0:T(8,128)(2,1)}, u32[]{:S(2)}) copy-start(bf16[512,2304]{1,0:T(8,128)(2,1)} %param.25) | copy-start | bytes 7077892
  7.2 261.2 %all-reduce.3.cloned.1.call-start = ((), (), s32[]{:S(2)}) async-start(), calls=%async_computation | async-start | bytes 18874368 | tf_op jit(solution)/shard_map/psum | solution.py:60
  10.2 13.8 %copy-start.8 = (f32[2304]{0:T(1024)}, f32[2304]{0:T(1024)S(1)}, u32[]{:S(2)}) copy-start(f32[2304]{0:T(1024)S(1)} %convert_add_fusion.6) | copy-start | bytes 27652
  13.5 5.7 copy-start.14
  23.9 4.4 copy-start.16
  38.8 0.8 copy-start.3
  38.8 1.0 copy-start.4
  44.1 26.7 %copy-start.15 = (f32[1024]{0:T(1024)S(1)}, f32[1024]{0:T(1024)}, u32[]{:S(2)}) copy-start(f32[1024]{0:T(1024)} %copy-done.14) | copy-start | bytes 12292
  70.8 4.3 copy-start.5
  70.8 4.3 copy-start.7
  83.5 5.2 copy-start.9
  83.5 5.2 copy-start.10
  88.6 420.3 %all-reduce.5.cloned.1.call-start = ((), (), s32[]{:S(2)}) async-start(), calls=%async_computation.1 | async-start | bytes 18874368 | tf_op jit(solution)/shard_map/psum | solution.py:67
  279.1 2.2 copy-start.2
  332.0 0.7 copy-start.11
  332.0 0.7 copy-start.12
  522.6 168.3 %copy-start.6 = (s32[32000]{0:T(1024)S(1)}, s32[32000]{0:T(1024)}, u32[]{:S(2)}) copy-start(s32[32000]{0:T(1024)} %iota_add_fusion) | copy-start | bytes 384004
  522.6 168.3 %copy-start.13 = (s32[1024]{0:T(1024)S(1)}, s32[1024]{0:T(1024)}, u32[]{:S(2)}) copy-start(s32[1024]{0:T(1024)} %param.20) | copy-start | bytes 12292
  691.0 71.1 %copy-start.1 = (bf16[512,2304]{1,0:T(8,128)(2,1)S(1)}, bf16[512,2304]{1,0:T(8,128)(2,1)}, u32[]{:S(2)}) copy-start(bf16[512,2304]{1,0:T(8,128)(2,1)} %param.25) | copy-start | bytes 7077892
Sparse Core Ops, SparseCore 0:
  88.8 179.5 all-reduce.2
  332.1 176.7 all-reduce.4
where the time goes:
time: 778 us; the launch traced here: 769 us
  waiting for transfers between devices  355 us (46%)
  matrix products  256 us (33%)
  other arithmetic  119 us (15%)
  between operations  14.8 us (2%)
  local copies, waits for them, and re-layouts  13.4 us (2%)
  blocking collectives  11.1 us (1%)
    psum x1, waiting for transfers between devices, local_step(): attn_out = lax.psum(attn_part, 't')  180 us
    psum x1, waiting for transfers between devices, local_step(): mlp_out = lax.psum(mlp_part, 't')  176 us
    dot_general x1, matrix products, local_step(): lax.dot_general(final_h, embed_table, (((1,), (1,)), ((), ())), preferred...  168 us
    reduce_sum x1, other arithmetic, local_step(): local_sum = jnp.sum(jnp.exp(capped - local_max[:, None]), axis=1)  59.2 us
    dot_general x1, matrix products, local_step(): mlp_part = jnp.dot(activated, w_down, preferred_element_type=jnp.float32)  35 us
    reduce_sum x5, other arithmetic, rms_norm(): jnp.mean(x_f32 * x_f32, axis=-1, keepdims=True) + NORM_EPS  27.7 us
    dot_general x1, matrix products, local_step(): gate_proj = jnp.dot(mlp_in, w_gate, preferred_element_type=jnp.float32)  15.7 us
  transfers between devices with their start and end apart: 2, of which 2 were waited for; matrix products, arithmetic and copies ran while one was open for 0% of the time, Pallas kernels for 0%

commit v1 on v0

v1 whole, which is shorter than its diff:
```python
import jax
import jax.numpy as jnp
import numpy as np
from jax import lax
from jax.experimental import pallas as pl
from jax.experimental.pallas import tpu as pltpu
from jax.sharding import PartitionSpec as P

ATTN_CAP = 50.0
FINAL_CAP = 30.0
NORM_EPS = 1e-6
ROPE_BASE = 10000.0
LOG2E = 1.4426950408889634
BF16 = jnp.bfloat16
F32 = jnp.float32
VMEM_LIMIT = 60 * 1024 * 1024
VMEM_MAX = 67043328


def rms_norm(values, gain_vec):
    x_f32 = values.astype(F32)
    scaled = x_f32 * lax.rsqrt(jnp.mean(x_f32 * x_f32, axis=-1, keepdims=True) + NORM_EPS)
    return scaled * (1.0 + gain_vec.astype(F32))


def rope(vec, cos_t, sin_t):
    low, high = vec[:, :128], vec[:, 128:]
    out = jnp.concatenate([low * cos_t - high * sin_t, high * cos_t + low * sin_t], axis=1)
    return out.astype(BF16).astype(F32)


def attn_kernel(half_ref, x_ref, len_ref, g_ref, freq_ref, wq_ref, wk_ref, wv_ref, wo_ref, kc_ref, vc_ref, p_ref, o_scr):
    tb = x_ref.shape[0]
    groups = tb // 8
    scale = 1.0 / (16.0 * ATTN_CAP)
    a = rms_norm(x_ref[...], g_ref[0:1, :]).astype(BF16)
    q = jnp.dot(a, wq_ref[...], preferred_element_type=F32)
    k = jnp.dot(a, wk_ref[...], preferred_element_type=F32)
    v = jnp.dot(a, wv_ref[...], preferred_element_type=F32).astype(BF16).astype(F32)
    lens = jnp.broadcast_to(len_ref[0], (8, tb)).T[:, :1]
    ang = lens.astype(F32) * freq_ref[...]
    cos_t, sin_t = jnp.cos(ang), jnp.sin(ang)

    def pairs(first, second):
        both = jnp.stack([first.reshape(groups, 8, -1), second.reshape(groups, 8, -1)], axis=1)
        return both.reshape(2 * tb, first.shape[1])

    q_all = pairs(rope(q[:, :256], cos_t, sin_t), rope(q[:, 256:], cos_t, sin_t))
    k = rope(k, cos_t, sin_t)
    k_all, v_all, len_all = pairs(k, k), pairs(v, v), pairs(lens, lens)
    q_b = q_all.astype(BF16)
    nt = (((1,), (1,)), ((), ()))
    s = jnp.concatenate([lax.dot_general(q_b[16 * i:16 * i + 16], kc_ref[256 * i:256 * i + 256, :], nt, preferred_element_type=F32)
                         for i in range(groups)], axis=0)
    s = ATTN_CAP * jnp.tanh(s * scale)
    row = lax.broadcasted_iota(jnp.int32, s.shape, 0)
    col = lax.broadcasted_iota(jnp.int32, s.shape, 1)
    rel = col - (row % 8) * 32
    s = jnp.where((rel >= 0) & (rel < len_all), s, -1e30)
    s_new = ATTN_CAP * jnp.tanh(jnp.sum(q_all * k_all, axis=1, keepdims=True) * scale)
    top = jnp.maximum(jnp.max(s, axis=1, keepdims=True), s_new)
    e = jnp.exp(s - top)
    e_new = jnp.exp(s_new - top)
    den = jnp.sum(e, axis=1, keepdims=True) + e_new
    e_b = e.astype(BF16)
    o = jnp.concatenate([jnp.dot(e_b[16 * i:16 * i + 16], vc_ref[256 * i:256 * i + 256, :], preferred_element_type=F32)
                         for i in range(groups)], axis=0)
    o = (o + e_new.astype(BF16).astype(F32) * v_all) / den
    for i in range(groups):
        o_scr[8 * i:8 * i + 8, :256] = o[16 * i:16 * i + 8]
        o_scr[8 * i:8 * i + 8, 256:] = o[16 * i + 8:16 * i + 16]
    o_b = o_scr[...].astype(BF16)
    mid = wo_ref.shape[1] // 2
    p_ref[0] = jnp.dot(o_b, wo_ref[:, :mid], preferred_element_type=F32)
    p_ref[1] = jnp.dot(o_b, wo_ref[:, mid:], preferred_element_type=F32)


def attention(half, x, lens, g, freq, wq, wk, wv, wo, kc, vc, tb=128):
    n = x.shape[0] // 2
    nb = n // tb
    d = x.shape[1]
    full = lambda s: pl.BlockSpec(s, lambda i, h: (0, 0))
    rows = lambda r, c: pl.BlockSpec((r, c), lambda i, h: (h[0] * nb + i, 0))
    return pl.pallas_call(
        attn_kernel,
        grid_spec=pltpu.PrefetchScalarGridSpec(
            num_scalar_prefetch=1, grid=(nb,),
            in_specs=[rows(tb, d), pl.BlockSpec((1, 1, tb), lambda i, h: (h[0] * nb + i, 0, 0)), full(g.shape), full(freq.shape), full(wq.shape), full(wk.shape),
                      full(wv.shape), full(wo.shape), rows(tb * 32, 256), rows(tb * 32, 256)],
            out_specs=pl.BlockSpec((2, tb, d // 2), lambda i, h: (0, i, 0)),
            scratch_shapes=[pltpu.VMEM((tb, 512), F32)]),
        out_shape=jax.ShapeDtypeStruct((2, n, d // 2), F32),
        compiler_params=pltpu.CompilerParams(vmem_limit_bytes=VMEM_LIMIT),
        name='attn',
    )(half, x, lens, g, freq, wq, wk, wv, wo, kc, vc)


MESH = pl.DeviceIdType.MESH
CHUNKS = 4
OWN = 128
PART = OWN // CHUNKS
COLS = 1152


def place():
    t, v = lax.axis_index('t'), lax.axis_index('v')
    return t, v, t + 1 - 2 * (t % 2), (t + 2) % 4, 3 - t


def meet_all(t, v):
    barrier = pltpu.get_barrier_semaphore()
    for dt in range(4):
        for dv in range(2):
            if dt or dv:
                pl.semaphore_signal(barrier, inc=1, device_id=((t + dt) % 4, (v + dv) % 2), device_id_type=MESH)
    pl.semaphore_wait(barrier, 7)


def send(src, dst, sems, idx, dev):
    return pltpu.make_async_remote_copy(src_ref=src, dst_ref=dst, send_sem=sems.at[(0,) + idx], recv_sem=sems.at[(1,) + idx],
                                        device_id=dev, device_id_type=MESH)


def norm_halves(h0, h1, g_ref):
    d = 2 * h0.shape[1]
    inv = lax.rsqrt((jnp.sum(h0 * h0, axis=1, keepdims=True) + jnp.sum(h1 * h1, axis=1, keepdims=True)) / d + NORM_EPS)
    return h0 * inv * (1.0 + g_ref[:, :COLS]), h1 * inv * (1.0 + g_ref[:, COLS:])


def layer_kernel(p1, x_hbm, gains, wg_hbm, wu_hbm, wd_hbm, y_ref,
                 wg, wu, wd, xb, x1, r1, r2, r3, r4, fwd, ag, p2, mb, act, loads, s1, s2, s3, s4, s5, s6):
    t, v, tx, ty, tz = place()
    dev_x, dev_y = (tx, v), (ty, v)
    g_post, g_pre, g_mlp = gains[1:2, :], gains[2:3, :], gains[3:4, :]
    rows = lambda q, c: pl.ds(pl.multiple_of(q * OWN + c * PART, PART), PART)
    part = lambda c: pl.ds(pl.multiple_of(c * PART, PART), PART)
    weights = [pltpu.make_async_copy(a, b, loads.at[i]) for i, (a, b) in enumerate(((wg_hbm, wg), (wu_hbm, wu), (wd_hbm, wd)))]
    x_load = pltpu.make_async_copy(x_hbm.at[pl.ds(pl.multiple_of((v * 4 + t) * OWN, OWN), OWN)], xb, loads.at[3])
    x_load.start()
    for w in weights:
        w.start()
    meet_all(t, v)

    def rs_first(p, r, sems, c):
        return [send(p.at[h, rows(q, c)], r.at[h, slot, part(c)], sems, (c, 2 * h + slot), dev)
                for h, slot, q, dev in ((0, 1, tz, dev_x), (1, 1, tz, dev_y), (0, 0, tx, dev_x), (1, 0, ty, dev_y))]

    def rs_second(r, sems, c):
        return [send(fwd.at[h, part(c)], r.at[h, part(c)], sems, (c, h), dev) for h, dev in ((0, dev_y), (1, dev_x))]

    def rs_forward(p, r, r_next, sems, sems_next, c):
        first = rs_first(p, r, sems, c)
        for h, q, cp in ((0, ty, rs_second(r_next, sems_next, c)[0]), (1, tx, rs_second(r_next, sems_next, c)[1])):
            first[h].wait_recv()
            fwd[h, part(c)] = p[h, rows(q, c)] + r[h, 1, part(c)]
            cp.start()

    def rs_finish(p, r, r_next, sems, sems_next, c):
        first, second = rs_first(p, r, sems, c), rs_second(r_next, sems_next, c)
        out = []
        for h in range(2):
            first[2 + h].wait_recv()
            second[h].wait_recv()
            out.append(p[h, rows(t, c)] + r[h, 0, part(c)] + r_next[h, part(c)])
        for cp in first + second:
            cp.wait_send()
        return out

    def ag_first(c):
        return [send(ag.at[h, rows(t, c)], ag.at[h, rows(t, c)], s3, (c, i), dev)
                for i, (h, dev) in enumerate(((0, dev_x), (1, dev_y), (1, dev_x), (0, dev_y)))]

    def ag_second(c):
        return [send(ag.at[h, rows(q, c)], ag.at[h, rows(q, c)], s4, (c, h), dev) for h, q, dev in ((0, tx, dev_y), (1, ty, dev_x))]

    def each(body):
        lax.fori_loop(0, CHUNKS, lambda c, _: (body(c), 0)[1], 0)

    @each
    def _(c):
        for cp in rs_first(p1, r1, s1, c):
            cp.start()

    @each
    def _(c):
        rs_forward(p1, r1, r2, s1, s2, c)

    x_load.wait()

    @each
    def _(c):
        s_a, s_b = norm_halves(*rs_finish(p1, r1, r2, s1, s2, c), g_post)
        x_a = (xb[part(c), :COLS].astype(F32) + s_a).astype(BF16)
        x_b = (xb[part(c), COLS:].astype(F32) + s_b).astype(BF16)
        x1[part(c), :COLS] = x_a
        x1[part(c), COLS:] = x_b
        m_a, m_b = norm_halves(x_a.astype(F32), x_b.astype(F32), g_pre)
        ag[0, rows(t, c)] = m_a.astype(BF16).astype(F32)
        ag[1, rows(t, c)] = m_b.astype(BF16).astype(F32)
        for cp in ag_first(c):
            cp.start()

    @each
    def _(c):
        for cp, nxt in zip(ag_first(c)[:2], ag_second(c)):
            cp.wait_recv()
            nxt.start()

    for w in weights:
        w.wait()

    @each
    def _(c):
        for cp in ag_first(c)[2:] + ag_second(c):
            cp.wait_recv()
        for q in range(4):
            for h in range(2):
                mb[PART * q:PART * q + PART, COLS * h:COLS * h + COLS] = ag[h, rows(q, c)].astype(BF16)

        def up(j, _):
            cols = pl.ds(pl.multiple_of(j * 256, 256), 256)
            gate = jnp.dot(mb[...], wg[:, cols], preferred_element_type=F32)
            lift = jnp.dot(mb[...], wu[:, cols], preferred_element_type=F32)
            act[:, cols] = (jax.nn.gelu(gate, approximate=True) * lift).astype(BF16)
            return 0

        lax.fori_loop(0, wg.shape[1] // 256, up, 0)
        for h in range(2):
            def down(j, _):
                res = jnp.dot(act[...], wd[:, pl.ds(pl.multiple_of(COLS * h + j * 384, 128), 384)], preferred_element_type=F32)
                for q in range(4):
                    p2[h, rows(q, c), pl.ds(pl.multiple_of(j * 384, 128), 384)] = res[PART * q:PART * q + PART]
                return 0

            lax.fori_loop(0, COLS // 384, down, 0)
        for cp in rs_first(p2, r3, s5, c):
            cp.start()

    @each
    def _(c):
        rs_forward(p2, r3, r4, s5, s6, c)

    @each
    def _(c):
        s_a, s_b = norm_halves(*rs_finish(p2, r3, r4, s5, s6, c), g_mlp)
        y_ref[0, part(c)] = (x1[part(c), :COLS].astype(F32) + s_a).astype(BF16).astype(F32)
        y_ref[1, part(c)] = (x1[part(c), COLS:].astype(F32) + s_b).astype(BF16).astype(F32)
        for cp in ag_first(c) + ag_second(c):
            cp.wait_send()


def layer(p1, x, gains, wg, wu, wd):
    d, f = wg.shape
    n = p1.shape[1]
    vm, hbm = pl.BlockSpec(memory_space=pltpu.VMEM), pl.BlockSpec(memory_space=pl.ANY)
    sem = lambda k: pltpu.SemaphoreType.DMA((2, CHUNKS, k))
    return pl.pallas_call(
        layer_kernel,
        out_shape=jax.ShapeDtypeStruct((2, OWN, COLS), F32),
        in_specs=[vm, hbm, vm, hbm, hbm, hbm],
        out_specs=vm,
        scratch_shapes=[
            pltpu.VMEM((d, f), BF16), pltpu.VMEM((d, f), BF16), pltpu.VMEM((f, d), BF16),
            pltpu.VMEM((OWN, d), BF16), pltpu.VMEM((OWN, d), BF16),
            pltpu.VMEM((2, 2, OWN, COLS), F32), pltpu.VMEM((2, OWN, COLS), F32),
            pltpu.VMEM((2, 2, OWN, COLS), F32), pltpu.VMEM((2, OWN, COLS), F32),
            pltpu.VMEM((2, OWN, COLS), F32), pltpu.VMEM((2, n, COLS), F32), pltpu.VMEM((2, n, COLS), F32),
            pltpu.VMEM((OWN, d), BF16), pltpu.VMEM((OWN, f), BF16),
            pltpu.SemaphoreType.DMA((4,)), sem(4), sem(2), sem(4), sem(2), sem(4), sem(2)],
        compiler_params=pltpu.CompilerParams(collective_id=0, has_side_effects=True, vmem_limit_bytes=VMEM_MAX),
        name='layer',
    )(p1, x, gains, wg, wu, wd)


TILE = 640
SLOTS = 3


def head_epilogue(logits, diff, base):
    tv, n = logits.shape
    th = jnp.tanh(logits * (1.0 / FINAL_CAP)).reshape(tv // 8, 8, n)
    ex = jnp.exp2(th * (FINAL_CAP * LOG2E))
    rows = lax.broadcasted_iota(jnp.int32, th.shape, 0) * 8
    hit = jnp.where((diff - base)[None] == rows, th, 0.0)
    return jnp.sum(ex, axis=0), jnp.sum(hit, axis=0)


def head_kernel(y_own, gains, tgt, e_hbm, y_out, lp_ref,
                ag, yb, ht, eb, lg_a, lg_b, dif, tot, hit, part, fin, e_sem, y_sem, s1, s2, s3, s4):
    t, v, tx, ty, tz = place()
    me = v * 4 + t
    dev_x, dev_y, dev_p = (tx, v), (ty, v), (t, 1 - v)
    chips = (t, tx, ty, tz)
    g_fin = gains[4:5, :]
    vocab = e_hbm.shape[0]
    pairs = vocab // (2 * TILE)
    total = 2 * pairs

    def fetch(g):
        src = e_hbm.at[pl.ds(pl.multiple_of((g % pairs) * (2 * TILE), 2 * TILE), 2 * TILE)]
        return pltpu.make_async_copy(src, eb.at[g % SLOTS], e_sem.at[g % SLOTS])

    for g in range(SLOTS - 1):
        fetch(g).start()
    meet_all(t, v)

    first = [send(y_own.at[h], ag.at[h, me], s1, (i,), dev)
             for i, (h, dev) in enumerate(((0, dev_x), (1, dev_y), (1, dev_x), (0, dev_y)))]
    second = [send(ag.at[h, v * 4 + q], ag.at[h, v * 4 + q], s2, (h,), dev) for h, q, dev in ((0, tx, dev_y), (1, ty, dev_x))]
    cross = [send(y_own, ag.at[:, me], s3, (0,), dev_p)]
    cross += [send(ag.at[:, v * 4 + q], ag.at[:, v * 4 + q], s3, (i + 1,), dev_p) for i, q in enumerate((tx, ty, tz))]
    cross[0].start()
    for cp in first:
        cp.start()
    tot[...] = jnp.zeros_like(tot)
    hit[...] = jnp.zeros_like(hit)
    for g, q in enumerate(chips):
        for w in range(2):
            lane = tgt[w * 4 + q] - me * vocab
            dif[g, :, 128 * w:128 * w + 128] = lane - lax.broadcasted_iota(jnp.int32, (8, 128), 0)

    def y_copy(b):
        return pltpu.make_async_copy(yb.at[b], y_out.at[pl.ds(pl.multiple_of(b * OWN, OWN), OWN)], y_sem.at[b])

    def prepare(src, b, g, w):
        h_a, h_b = src(0), src(1)
        yb[b, :, :COLS] = h_a.astype(BF16)
        yb[b, :, COLS:] = h_b.astype(BF16)
        y_copy(b).start()
        n_a, n_b = norm_halves(h_a, h_b, g_fin)
        ht[g, :COLS, 128 * w:128 * w + 128] = n_a.T.astype(BF16)
        ht[g, COLS:, 128 * w:128 * w + 128] = n_b.T.astype(BF16)

    def prepare_chip(g, q):
        for w in range(2):
            prepare(lambda h: ag[h, w * 4 + q], w * 4 + q, g, w)

    def mine(h):
        return y_own[h]

    cross[0].wait_recv()
    for w in range(2):
        @pl.when(v == w)
        def _():
            prepare(mine, me, 0, w)
            prepare(lambda h: ag[h, (1 - w) * 4 + t], (1 - w) * 4 + t, 0, 1 - w)

    def epilogue(lg, g, base, valid):
        s, k = head_epilogue(lg[...], dif[g], base)
        tot[g] += jnp.where(valid, s, 0.0)
        hit[g] += jnp.where(valid, k, 0.0)

    def body(i, offset, groups):
        g = i + offset
        slot = g % SLOTS
        fetch(g).wait()

        @pl.when(g + SLOTS - 1 < total)
        def _():
            fetch(g + SLOTS - 1).start()

        last = (groups[-1], (2 * i - 1) * TILE, i > 0)
        bufs = (lg_a, lg_b)
        count = 0
        for k in range(2):
            for grp in groups:
                cur, prev = bufs[count % 2], bufs[(count + 1) % 2]
                cur[...] = jnp.dot(eb[slot, TILE * k:TILE * k + TILE, :], ht[grp], preferred_element_type=F32)
                epilogue(prev, *last)
                last = (grp, (2 * i + k) * TILE, True)
                count += 1

    def pass_one(i, _):
        @pl.when(i == 9)
        def _():
            for cp, nxt in zip(first[:2], second):
                cp.wait_recv()
                nxt.start()

        @pl.when(i == 18)
        def _():
            for cp in first[2:]:
                cp.wait_recv()
            cross[1].start()
            cross[2].start()

        body(i, 0, (0,))
        return 0

    lax.fori_loop(0, pairs, pass_one, 0)
    epilogue(lg_b, 0, (2 * pairs - 1) * TILE, True)
    for cp in second:
        cp.wait_recv()
    cross[3].start()
    for g in (1, 2, 3):
        cross[g].wait_recv()
        prepare_chip(g, chips[g])
    lax.fori_loop(0, pairs, lambda i, _: (body(i, pairs, (1, 2, 3)), 0)[1], 0)
    epilogue(lg_b, 3, (2 * pairs - 1) * TILE, True)

    for g, q in enumerate(chips):
        for w in range(2):
            lanes = slice(128 * w, 128 * w + 128)
            part[w * 4 + q, 0:1] = jnp.sum(tot[g, :, lanes], axis=0, keepdims=True)
            part[w * 4 + q, 1:2] = jnp.sum(hit[g, :, lanes], axis=0, keepdims=True)
    outs = []
    for k in range(1, 8):
        dt, dv = k % 4, k // 4
        outs.append(send(part, fin.at[k], s4, (k - 1,), ((t + dt) % 4, (v + dv) % 2)))
    for cp in outs:
        cp.start()
    acc = part[...]
    for k in range(1, 8):
        outs[k - 1].wait_recv()
        acc += fin[k]
    lp_ref[...] = FINAL_CAP * acc[:, 1] - jnp.log(acc[:, 0])
    for cp in first + second + cross + outs:
        cp.wait_send()
    for b in range(8):
        y_copy(b).wait()


def head(y_own, gains, tgt, table):
    d = table.shape[1]
    vm, hbm = pl.BlockSpec(memory_space=pltpu.VMEM), pl.BlockSpec(memory_space=pl.ANY)
    return pl.pallas_call(
        head_kernel,
        out_shape=[jax.ShapeDtypeStruct((8 * OWN, d), BF16), jax.ShapeDtypeStruct((8, OWN), F32)],
        in_specs=[vm, vm, vm, hbm],
        out_specs=[hbm, vm],
        scratch_shapes=[
            pltpu.VMEM((2, 8, OWN, COLS), F32), pltpu.VMEM((8, OWN, d), BF16), pltpu.VMEM((4, d, 256), BF16),
            pltpu.VMEM((SLOTS, 2 * TILE, d), BF16), pltpu.VMEM((TILE, 256), F32), pltpu.VMEM((TILE, 256), F32),
            pltpu.VMEM((4, 8, 256), jnp.int32), pltpu.VMEM((4, 8, 256), F32), pltpu.VMEM((4, 8, 256), F32),
            pltpu.VMEM((8, 2, OWN), F32), pltpu.VMEM((8, 8, 2, OWN), F32),
            pltpu.SemaphoreType.DMA((SLOTS,)), pltpu.SemaphoreType.DMA((8,)),
            pltpu.SemaphoreType.DMA((2, 4)), pltpu.SemaphoreType.DMA((2, 2)), pltpu.SemaphoreType.DMA((2, 4)), pltpu.SemaphoreType.DMA((2, 7))],
        compiler_params=pltpu.CompilerParams(collective_id=1, has_side_effects=True, vmem_limit_bytes=VMEM_MAX),
        name='head',
    )(y_own, gains, tgt, table)


def solution(mesh):
    in_specs = (P(), P(), P(), P(), P(None, 't'), P(None, 't'), P(None, 't'), P('t', None), P(), P(), P(None, 't'), P(None, 't'), P('t', None), P(), P(), P(None, None, 't', None), P(None, None, 't', None), P(('v', 't'), None))

    def local_step(hidden_in, seq_lens, target, g_attn_pre, w_q, w_k, w_v, w_o, g_attn_post, g_mlp_pre, w_gate, w_up, w_down, g_mlp_post, g_final, k_cache, v_cache, embed_table):
        half = lax.axis_index('v')
        gains = jnp.stack([g_attn_pre, g_attn_post, g_mlp_pre, g_mlp_post, g_final]).astype(F32)
        freq = jnp.asarray((ROPE_BASE ** (-2.0 * np.arange(128, dtype=np.float32) / 256)).astype(np.float32)[None])
        p1 = attention(half[None].astype(jnp.int32), hidden_in, seq_lens.reshape(-1, 1, 128), gains, freq, w_q, w_k, w_v, w_o,
                       k_cache.reshape(-1, 256), v_cache.reshape(-1, 256))
        y_own = layer(p1, hidden_in, gains, w_gate, w_up, w_down)
        hidden_out, logprob = head(y_own, gains, target.reshape(8, 1, OWN), embed_table)
        return logprob.reshape(-1), hidden_out

    return jax.shard_map(local_step, mesh=mesh, in_specs=in_specs, out_specs=(P(), P()), check_vma=False)
```

time: 778 us -> 336 us (0.43); the launches traced: 769 us -> 336 us
  waiting for transfers between devices: 355 us -> 0 us
  Pallas kernels: 0 us -> 325 us
  matrix products: 256 us -> 0 us
  other arithmetic: 119 us -> 0.63 us
  between operations: 14.8 us -> 0.66 us
  blocking collectives: 11.1 us -> 0 us
    psum x2 -> x0, waiting for transfers between devices: 355 us -> none  [the longest x1 180 us: local_step(): attn_out = lax.psum(attn_part, 't')]
    pallas_call x0 -> x3, Pallas kernels: none -> 325 us  [the longest x1 181 us: head(): pl.pallas_call(head_kernel, out_shape=[jax.ShapeDtypeStruct((8 * OWN, d),...]
    dot_general x9 -> x0, matrix products: 256 us -> none  [the longest x1 168 us: local_step(): lax.dot_general(final_h, embed_table, (((1,), (1,)), ((), ())), preferred...]
    reduce_sum x9 -> x0, other arithmetic: 103 us -> none  [the longest x1 59.2 us: local_step(): local_sum = jnp.sum(jnp.exp(capped - local_max[:, None]), axis=1)]
    all_gather x1 -> x0, blocking collectives: 11.1 us -> none  [local_step(): lax.all_gather(jnp.stack([local_max, local_sum, local_tgt]), ('v', 't'))]
  transfers between devices with their start and end apart: 2 -> 0, of which waited for: 2 -> 0; matrix products, arithmetic and copies ran while one was open for 0% -> 0% of each run, Pallas kernels for 0% -> 0%
where the time goes in v1:
time: 336 us
  Pallas kernels  325 us (97%)
  local copies, waits for them, and re-layouts  9.67 us (3%)
    pallas_call x1, Pallas kernels, head(): pl.pallas_call(head_kernel, out_shape=[jax.ShapeDtypeStruct((8 * OWN, d),...  181 us
    pallas_call x1, Pallas kernels, layer(): pl.pallas_call(layer_kernel, out_shape=jax.ShapeDtypeStruct((2, OWN, COLS...  128 us
    pallas_call x1, Pallas kernels, attention(): pl.pallas_call(attn_kernel, grid_spec=pltpu.PrefetchScalarGridSpec(num_sc...  15.6 us

profile of v1, /device:TPU:0, one launch (start us, length us, event | category | flops | bytes accessed | tf_op | source)
XLA Modules:
  0.0 336.1 jit_solution(7254575436235306540)
XLA Ops:
  0.6 0.7 stack.18
  1.3 0.7 stack.19
  2.0 0.7 stack.20
  2.7 0.7 stack.21
  3.4 0.7 stack.22
  4.1 0.1 stack.23
  4.2 0.6 convert_element_type.3.g_ref.gains
  4.8 15.6 %attn.1.p1 = f32[2,512,1152]{2,1,0:T(8,128)} custom-call(s32[1]{0:T(128)} %bitcast.half_ref, bf16[1024,2304]{1,0:T(8,128)(2,1)} %x_hbm.1, s32[8,1,128]{2,1,0:T(1,128)} %bitcast.9, f32[5,2304]{1,0:T(8,128)} %convert_element_type.3.g_ref.gains, f32[1,128]{1,0:T(1,128)} %constant.6.clone.freq_ref, bf16[2304,512]{1,0:T(8,128)(2,1)} %wq_ref.1, ...), custom_call_target="tpu_custom_call" | custom-call | tf_op jit(solution)/shard_map/attn/pallas_call | solution.py:84
  20.4 128.1 %layer.1.y_own = f32[2,128,1152]{2,1,0:T(8,128)} custom-call(f32[2,512,1152]{2,1,0:T(8,128)} %attn.1.p1, bf16[1024,2304]{1,0:T(8,128)(2,1)} %x_hbm.1, f32[5,2304]{1,0:T(8,128)} %convert_element_type.3.g_ref.gains, bf16[2304,2304]{1,0:T(8,128)(2,1)} %wg_hbm.1, bf16[2304,2304]{1,0:T(8,128)(2,1)} %wu_hbm.1, bf16[2304,2304]{1,0:T(8,128)(2,1)} %wd_hbm.1), custom_call_target="tpu_custom_call" | custom-call | tf_op jit(solution)/shard_map/layer/pallas_call | solution.py:257
  148.6 181.4 %head.1 = (bf16[1024,2304]{1,0:T(8,128)(2,1)}, f32[8,128]{1,0:T(8,128)}) custom-call(f32[2,128,1152]{2,1,0:T(8,128)} %layer.1.y_own, f32[5,2304]{1,0:T(8,128)} %convert_element_type.3.g_ref.gains, s32[8,1,128]{2,1,0:T(1,128)} %bitcast.8, bf16[32000,2304]{1,0:T(8,128)(2,1)} %e_hbm.1), custom_call_target="tpu_custom_call" | custom-call | tf_op jit(solution)/shard_map/head/pallas_call | solution.py:426
  330.0 1.3 copy.23
  331.3 4.8 %copy.24 = bf16[1024,2304]{1,0:T(8,128)(2,1)} copy(bf16[1024,2304]{1,0:T(8,128)(2,1)} %get-tuple-element.9) | data formatting | bytes 9437184

commit v2 on v1

v2 whole, which is shorter than its diff:
```python
import jax
import jax.numpy as jnp
import numpy as np
from jax import lax
from jax.experimental import pallas as pl
from jax.experimental.pallas import tpu as pltpu
from jax.sharding import PartitionSpec as P

ATTN_CAP = 50.0
FINAL_CAP = 30.0
NORM_EPS = 1e-6
ROPE_BASE = 10000.0
LOG2E = 1.4426950408889634
BF16 = jnp.bfloat16
F32 = jnp.float32
VMEM_LIMIT = 60 * 1024 * 1024
VMEM_MAX = 67043328


def rms_norm(values, gain_vec):
    x_f32 = values.astype(F32)
    scaled = x_f32 * lax.rsqrt(jnp.mean(x_f32 * x_f32, axis=-1, keepdims=True) + NORM_EPS)
    return scaled * (1.0 + gain_vec.astype(F32))


def rope(vec, cos_t, sin_t):
    low, high = vec[:, :128], vec[:, 128:]
    out = jnp.concatenate([low * cos_t - high * sin_t, high * cos_t + low * sin_t], axis=1)
    return out.astype(BF16).astype(F32)


def attend(x, lens, gain, freq, wq, wk, wv, wo, keys, vals, put):
    tb = x.shape[0]
    groups = tb // 8
    scale = 1.0 / (16.0 * ATTN_CAP)
    a = rms_norm(x, gain).astype(BF16)
    q = jnp.dot(a, wq, preferred_element_type=F32)
    k = jnp.dot(a, wk, preferred_element_type=F32)
    v = jnp.dot(a, wv, preferred_element_type=F32).astype(BF16).astype(F32)
    ang = lens.astype(F32) * freq
    cos_t, sin_t = jnp.cos(ang), jnp.sin(ang)

    def pairs(first, second):
        both = jnp.stack([first.reshape(groups, 8, -1), second.reshape(groups, 8, -1)], axis=1)
        return both.reshape(2 * tb, first.shape[1])

    q_all = pairs(rope(q[:, :256], cos_t, sin_t), rope(q[:, 256:], cos_t, sin_t))
    k = rope(k, cos_t, sin_t)
    k_all, v_all, len_all = pairs(k, k), pairs(v, v), pairs(lens, lens)
    q_b = q_all.astype(BF16)
    nt = (((1,), (1,)), ((), ()))
    s = jnp.concatenate([lax.dot_general(q_b[16 * i:16 * i + 16], keys(i), nt, preferred_element_type=F32)
                         for i in range(groups)], axis=0)
    s = ATTN_CAP * jnp.tanh(s * scale)
    row = lax.broadcasted_iota(jnp.int32, s.shape, 0)
    col = lax.broadcasted_iota(jnp.int32, s.shape, 1)
    rel = col - (row % 8) * 32
    s = jnp.where((rel >= 0) & (rel < len_all), s, -1e30)
    s_new = ATTN_CAP * jnp.tanh(jnp.sum(q_all * k_all, axis=1, keepdims=True) * scale)
    top = jnp.maximum(jnp.max(s, axis=1, keepdims=True), s_new)
    e = jnp.exp(s - top)
    e_new = jnp.exp(s_new - top)
    den = jnp.sum(e, axis=1, keepdims=True) + e_new
    e_b = e.astype(BF16)
    o = jnp.concatenate([jnp.dot(e_b[16 * i:16 * i + 16], vals(i), preferred_element_type=F32) for i in range(groups)], axis=0)
    o = ((o + e_new.astype(BF16).astype(F32) * v_all) / den).reshape(groups, 2, 8, 256)
    o_b = jnp.concatenate([o[:, 0].reshape(tb, 256), o[:, 1].reshape(tb, 256)], axis=1).astype(BF16)
    for j in range(wo.shape[1] // 384):
        put(j, jnp.dot(o_b, wo[:, 384 * j:384 * j + 384], preferred_element_type=F32))


MESH = pl.DeviceIdType.MESH
CHUNKS = 4
OWN = 128
PART = OWN // CHUNKS
COLS = 1152


def place():
    t, v = lax.axis_index('t'), lax.axis_index('v')
    return t, v, t + 1 - 2 * (t % 2), (t + 2) % 4, 3 - t


def meet_all(t, v):
    barrier = pltpu.get_barrier_semaphore()
    for dt in range(4):
        for dv in range(2):
            if dt or dv:
                pl.semaphore_signal(barrier, inc=1, device_id=((t + dt) % 4, (v + dv) % 2), device_id_type=MESH)
    pl.semaphore_wait(barrier, 7)


def send(src, dst, sems, idx, dev):
    return pltpu.make_async_remote_copy(src_ref=src, dst_ref=dst, send_sem=sems.at[(0,) + idx], recv_sem=sems.at[(1,) + idx],
                                        device_id=dev, device_id_type=MESH)


def norm_halves(h0, h1, g_ref):
    d = 2 * h0.shape[1]
    inv = lax.rsqrt((jnp.sum(h0 * h0, axis=1, keepdims=True) + jnp.sum(h1 * h1, axis=1, keepdims=True)) / d + NORM_EPS)
    return h0 * inv * (1.0 + g_ref[:, :COLS]), h1 * inv * (1.0 + g_ref[:, COLS:])


def layer_kernel(x_hbm, lens, gains, freq, wq_hbm, wk_hbm, wv_hbm, wo_hbm, kc_hbm, vc_hbm, wg_hbm, wu_hbm, wd_hbm, y_ref,
                 bank, xh, x1, p1, r1, r2, r3, r4, fwd, ag, p2, mb, act, lens_s, loads, caches, s1, s2, s3, s4, s5, s6):
    t, v, tx, ty, tz = place()
    dev_x, dev_y = (tx, v), (ty, v)
    g_post, g_pre, g_mlp = gains[1:2, :], gains[2:3, :], gains[3:4, :]
    d = xh.shape[1]
    rows = lambda q, c: pl.ds(pl.multiple_of(q * OWN + c * PART, PART), PART)
    part = lambda c: pl.ds(pl.multiple_of(c * PART, PART), PART)
    wq, wk, wv, wo = bank.at[:d, :512], bank.at[:d, 512:768], bank.at[:d, 768:1024], bank.at[d:d + 512]
    cache_row = d + 512
    wg, wu, wd = bank.at[:d], bank.at[d:2 * d], bank.at[2 * d:]
    local = pltpu.make_async_copy
    early = [local(a, b, loads.at[i]) for i, (a, b) in enumerate((
        (x_hbm.at[pl.ds(pl.multiple_of(v * 4 * OWN, 4 * OWN), 4 * OWN)], xh), (wq_hbm, wq), (wk_hbm, wk), (wv_hbm, wv)))]
    wo_load = local(wo_hbm, wo, loads.at[4])
    weights = [local(a, b, loads.at[5 + i]) for i, (a, b) in enumerate(((wg_hbm, wg), (wu_hbm, wu), (wd_hbm, wd)))]

    def cache_load(c):
        out = []
        for i, src in enumerate((kc_hbm, vc_hbm)):
            for q in range(4):
                first = pl.multiple_of(((v * 4 + q) * OWN + c * PART) * 32, PART * 32)
                out.append(local(src.at[pl.ds(first, PART * 32)],
                                 bank.at[pl.ds(cache_row + q * PART * 32, PART * 32), pl.ds(pl.multiple_of((2 * c + i) * 256, 256), 256)],
                                 caches.at[c, 4 * i + q]))
        return out

    for cp in early:
        cp.start()
    for cp in cache_load(0):
        cp.start()
    wo_load.start()
    for c in range(1, CHUNKS):
        for cp in cache_load(c):
            cp.start()
    for q in range(4):
        lens_s[OWN * q:OWN * q + OWN, :] = jnp.broadcast_to(lens[v * 4 + q], (OWN, OWN)).T
    meet_all(t, v)
    for cp in early:
        cp.wait()

    def rs_first(p, r, sems, c):
        return [send(p.at[h, rows(q, c)], r.at[h, slot, part(c)], sems, (c, 2 * h + slot), dev)
                for h, slot, q, dev in ((0, 1, tz, dev_x), (1, 1, tz, dev_y), (0, 0, tx, dev_x), (1, 0, ty, dev_y))]

    def rs_second(r, sems, c):
        return [send(fwd.at[h, part(c)], r.at[h, part(c)], sems, (c, h), dev) for h, dev in ((0, dev_y), (1, dev_x))]

    def rs_forward(p, r, r_next, sems, sems_next, c):
        first = rs_first(p, r, sems, c)
        for h, q, cp in ((0, ty, rs_second(r_next, sems_next, c)[0]), (1, tx, rs_second(r_next, sems_next, c)[1])):
            first[h].wait_recv()
            fwd[h, part(c)] = p[h, rows(q, c)] + r[h, 1, part(c)]
            cp.start()

    def rs_finish(p, r, r_next, sems, sems_next, c):
        first, second = rs_first(p, r, sems, c), rs_second(r_next, sems_next, c)
        out = []
        for h in range(2):
            first[2 + h].wait_recv()
            second[h].wait_recv()
            out.append(p[h, rows(t, c)] + r[h, 0, part(c)] + r_next[h, part(c)])
        for cp in first + second:
            cp.wait_send()
        return out

    def ag_first(c):
        return [send(ag.at[h, rows(t, c)], ag.at[h, rows(t, c)], s3, (c, i), dev)
                for i, (h, dev) in enumerate(((0, dev_x), (1, dev_y), (1, dev_x), (0, dev_y)))]

    def ag_second(c):
        return [send(ag.at[h, rows(q, c)], ag.at[h, rows(q, c)], s4, (c, h), dev) for h, q, dev in ((0, tx, dev_y), (1, ty, dev_x))]

    def each(body):
        lax.fori_loop(0, CHUNKS, lambda c, _: (body(c), 0)[1], 0)

    @each
    def _(c):
        for cp in cache_load(c):
            cp.wait()

        @pl.when(c == 0)
        def _():
            wo_load.wait()

        x = jnp.concatenate([xh[rows(q, c), :] for q in range(4)], axis=0)
        lens_c = jnp.concatenate([lens_s[rows(q, c), :1] for q in range(4)], axis=0)

        def cached(i):
            return lambda g: bank[pl.ds(cache_row + 256 * g, 256), pl.ds(pl.multiple_of((2 * c + i) * 256, 256), 256)]

        def put(j, res):
            h, first = j // 3, 384 * (j % 3)
            for q in range(4):
                p1[h, rows(q, c), first:first + 384] = res[PART * q:PART * q + PART]

        attend(x, lens_c, gains[0:1, :], freq[...], wq[...], wk[...], wv[...], wo, cached(0), cached(1), put)
        for cp in rs_first(p1, r1, s1, c):
            cp.start()

    for w in weights:
        w.start()

    @each
    def _(c):
        rs_forward(p1, r1, r2, s1, s2, c)

    @each
    def _(c):
        s_a, s_b = norm_halves(*rs_finish(p1, r1, r2, s1, s2, c), g_post)
        x_a = (xh[rows(t, c), :COLS].astype(F32) + s_a).astype(BF16)
        x_b = (xh[rows(t, c), COLS:].astype(F32) + s_b).astype(BF16)
        x1[part(c), :COLS] = x_a
        x1[part(c), COLS:] = x_b
        m_a, m_b = norm_halves(x_a.astype(F32), x_b.astype(F32), g_pre)
        ag[0, rows(t, c)] = m_a.astype(BF16).astype(F32)
        ag[1, rows(t, c)] = m_b.astype(BF16).astype(F32)
        for cp in ag_first(c):
            cp.start()

    @each
    def _(c):
        for cp, nxt in zip(ag_first(c)[:2], ag_second(c)):
            cp.wait_recv()
            nxt.start()

    for w in weights:
        w.wait()

    @each
    def _(c):
        for cp in ag_first(c)[2:] + ag_second(c):
            cp.wait_recv()
        for q in range(4):
            for h in range(2):
                mb[PART * q:PART * q + PART, COLS * h:COLS * h + COLS] = ag[h, rows(q, c)].astype(BF16)

        def up(j, _):
            cols = pl.ds(pl.multiple_of(j * 256, 256), 256)
            gate = jnp.dot(mb[...], wg[:, cols], preferred_element_type=F32)
            lift = jnp.dot(mb[...], wu[:, cols], preferred_element_type=F32)
            act[:, cols] = (jax.nn.gelu(gate, approximate=True) * lift).astype(BF16)
            return 0

        lax.fori_loop(0, d // 256, up, 0)
        for h in range(2):
            def down(j, _):
                res = jnp.dot(act[...], wd[:, pl.ds(pl.multiple_of(COLS * h + j * 384, 128), 384)], preferred_element_type=F32)
                for q in range(4):
                    p2[h, rows(q, c), pl.ds(pl.multiple_of(j * 384, 128), 384)] = res[PART * q:PART * q + PART]
                return 0

            lax.fori_loop(0, COLS // 384, down, 0)
        for cp in rs_first(p2, r3, s5, c):
            cp.start()

    @each
    def _(c):
        rs_forward(p2, r3, r4, s5, s6, c)

    @each
    def _(c):
        s_a, s_b = norm_halves(*rs_finish(p2, r3, r4, s5, s6, c), g_mlp)
        y_ref[0, part(c)] = (x1[part(c), :COLS].astype(F32) + s_a).astype(BF16).astype(F32)
        y_ref[1, part(c)] = (x1[part(c), COLS:].astype(F32) + s_b).astype(BF16).astype(F32)
        for cp in ag_first(c) + ag_second(c):
            cp.wait_send()


def layer(x, lens, gains, freq, wq, wk, wv, wo, kc, vc, wg, wu, wd):
    d = x.shape[1]
    n = x.shape[0] // 2
    vm, hbm = pl.BlockSpec(memory_space=pltpu.VMEM), pl.BlockSpec(memory_space=pl.ANY)
    sem = lambda k: pltpu.SemaphoreType.DMA((2, CHUNKS, k))
    return pl.pallas_call(
        layer_kernel,
        out_shape=jax.ShapeDtypeStruct((2, OWN, COLS), F32),
        in_specs=[hbm, vm, vm, vm] + [hbm] * 9,
        out_specs=vm,
        scratch_shapes=[
            pltpu.VMEM((3 * d, d), BF16), pltpu.VMEM((n, d), BF16), pltpu.VMEM((OWN, d), BF16), pltpu.VMEM((2, n, COLS), F32),
            pltpu.VMEM((2, 2, OWN, COLS), F32), pltpu.VMEM((2, OWN, COLS), F32),
            pltpu.VMEM((2, 2, OWN, COLS), F32), pltpu.VMEM((2, OWN, COLS), F32),
            pltpu.VMEM((2, OWN, COLS), F32), pltpu.VMEM((2, n, COLS), F32), pltpu.VMEM((2, n, COLS), F32),
            pltpu.VMEM((OWN, d), BF16), pltpu.VMEM((OWN, d), BF16), pltpu.VMEM((n, 128), jnp.int32),
            pltpu.SemaphoreType.DMA((8,)), pltpu.SemaphoreType.DMA((CHUNKS, 8)),
            sem(4), sem(2), sem(4), sem(2), sem(4), sem(2)],
        compiler_params=pltpu.CompilerParams(collective_id=0, has_side_effects=True, vmem_limit_bytes=VMEM_MAX),
        name='layer',
    )(x, lens, gains, freq, wq, wk, wv, wo, kc, vc, wg, wu, wd)


TILE = 1280
SUB = 320
SLOTS = 3


def head_epilogue(logits, diff, base):
    tv, n = logits.shape
    th = jnp.tanh(logits * (1.0 / FINAL_CAP)).reshape(tv // 8, 8, n)
    ex = jnp.exp2(th * (FINAL_CAP * LOG2E))
    rows = lax.broadcasted_iota(jnp.int32, th.shape, 0) * 8
    hit = jnp.where((diff - base)[None] == rows, th, 0.0)
    return jnp.sum(ex, axis=0), jnp.sum(hit, axis=0)


def head_kernel(y_own, gains, tgt, e_hbm, y_out, lp_ref,
                ag, yb, ht0, ht1, eb, lg_a, lg_b, dif, tot, hit, part, fin, e_sem, y_sem, s1, s2, s3, s4):
    t, v, tx, ty, tz = place()
    me = v * 4 + t
    dev_x, dev_y, dev_p = (tx, v), (ty, v), (t, 1 - v)
    g_fin = gains[4:5, :]
    tiles = e_hbm.shape[0] // TILE
    total = 2 * tiles

    def fetch(g):
        src = e_hbm.at[pl.ds(pl.multiple_of((g % tiles) * TILE, TILE), TILE)]
        return pltpu.make_async_copy(src, eb.at[g % SLOTS], e_sem.at[g % SLOTS])

    for g in range(SLOTS - 1):
        fetch(g).start()
    meet_all(t, v)

    first = [send(y_own.at[h], ag.at[h, me], s1, (i,), dev)
             for i, (h, dev) in enumerate(((0, dev_x), (1, dev_y), (1, dev_x), (0, dev_y)))]
    second = [send(ag.at[h, v * 4 + q], ag.at[h, v * 4 + q], s2, (h,), dev) for h, q, dev in ((0, tx, dev_y), (1, ty, dev_x))]
    cross = [send(y_own, ag.at[:, me], s3, (0,), dev_p)]
    cross += [send(ag.at[:, v * 4 + q], ag.at[:, v * 4 + q], s3, (i + 1,), dev_p) for i, q in enumerate((tx, ty, tz))]
    cross[0].start()
    for cp in first:
        cp.start()
    tot[...] = jnp.zeros_like(tot)
    hit[...] = jnp.zeros_like(hit)
    spots = [w * 4 + q for q in (t, tx, ty, tz) for w in range(2)]
    for k, b in enumerate(spots):
        lane = tgt[b] - me * e_hbm.shape[0]
        dif[:, OWN * k:OWN * k + OWN] = lane - lax.broadcasted_iota(jnp.int32, (8, OWN), 0)

    def y_copy(b):
        return pltpu.make_async_copy(yb.at[b], y_out.at[pl.ds(pl.multiple_of(b * OWN, OWN), OWN)], y_sem.at[b])

    def prepare(h_a, h_b, b, ht, lanes):
        yb[b, :, :COLS] = h_a.astype(BF16)
        yb[b, :, COLS:] = h_b.astype(BF16)
        y_copy(b).start()
        n_a, n_b = norm_halves(h_a, h_b, g_fin)
        ht[:COLS, lanes] = n_a.T.astype(BF16)
        ht[COLS:, lanes] = n_b.T.astype(BF16)

    cross[0].wait_recv()
    other = (1 - v) * 4 + t
    prepare(y_own[0], y_own[1], me, ht0, pl.ds(pl.multiple_of(v * OWN, OWN), OWN))
    prepare(ag[0, other], ag[1, other], other, ht0, pl.ds(pl.multiple_of((1 - v) * OWN, OWN), OWN))

    def epilogue(lg, span, base, valid):
        s, k = head_epilogue(lg, dif[:, span], base)
        tot[:, span] += jnp.where(valid, s, 0.0)
        hit[:, span] += jnp.where(valid, k, 0.0)

    def body(i, offset, ht, bufs, span):
        g = i + offset
        slot = g % SLOTS
        fetch(g).wait()

        @pl.when(g + SLOTS - 1 < total)
        def _():
            fetch(g + SLOTS - 1).start()

        for k in range(TILE // SUB):
            cur, prev = bufs[k % 2], bufs[(k + 1) % 2]
            cur[...] = jnp.dot(eb[slot, SUB * k:SUB * k + SUB, :], ht[...], preferred_element_type=F32)
            epilogue(prev[...], span, i * TILE + (k - 1) * SUB, True if k else i > 0)

    near, far = slice(0, 2 * OWN), slice(2 * OWN, 8 * OWN)
    near_bufs = (lg_a.at[:, near], lg_b.at[:, near])

    def pass_one(i, _):
        @pl.when(i == 9)
        def _():
            for cp, nxt in zip(first[:2], second):
                cp.wait_recv()
                nxt.start()

        @pl.when(i == 15)
        def _():
            for cp in first[2:]:
                cp.wait_recv()
            cross[1].start()
            cross[2].start()

        @pl.when(i == 17)
        def _():
            cross[1].wait_recv()
            cross[2].wait_recv()

        @pl.when((i >= 17) & (i < 21))
        def _():
            k = i - 17
            chip = tx + (k // 2) * (ty - tx)
            b = (k % 2) * 4 + chip
            prepare(ag[0, b], ag[1, b], b, ht1, pl.ds(pl.multiple_of(k * OWN, OWN), OWN))

        @pl.when(i == 23)
        def _():
            for cp in second:
                cp.wait_recv()
            cross[3].start()

        body(i, 0, ht0, near_bufs, near)
        return 0

    lax.fori_loop(0, tiles, pass_one, 0)
    epilogue(lg_b[:, near], near, tiles * TILE - SUB, True)
    cross[3].wait_recv()
    for k in (4, 5):
        b = (k % 2) * 4 + tz
        prepare(ag[0, b], ag[1, b], b, ht1, slice(OWN * k, OWN * k + OWN))
    lax.fori_loop(0, tiles, lambda i, _: (body(i, tiles, ht1, (lg_a, lg_b), far), 0)[1], 0)
    epilogue(lg_b[...], far, tiles * TILE - SUB, True)

    for k, b in enumerate(spots):
        lanes = slice(OWN * k, OWN * k + OWN)
        part[b, 0:1] = jnp.sum(tot[:, lanes], axis=0, keepdims=True)
        part[b, 1:2] = jnp.sum(hit[:, lanes], axis=0, keepdims=True)
    outs = []
    for k in range(1, 8):
        dt, dv = k % 4, k // 4
        outs.append(send(part, fin.at[k], s4, (k - 1,), ((t + dt) % 4, (v + dv) % 2)))
    for cp in outs:
        cp.start()
    acc = part[...]
    for k in range(1, 8):
        outs[k - 1].wait_recv()
        acc += fin[k]
    lp_ref[...] = FINAL_CAP * acc[:, 1] - jnp.log(acc[:, 0])
    for cp in first + second + cross + outs:
        cp.wait_send()
    for b in range(8):
        y_copy(b).wait()


def head(y_own, gains, tgt, table):
    d = table.shape[1]
    vm, hbm = pl.BlockSpec(memory_space=pltpu.VMEM), pl.BlockSpec(memory_space=pl.ANY)
    return pl.pallas_call(
        head_kernel,
        out_shape=[jax.ShapeDtypeStruct((8 * OWN, d), BF16), jax.ShapeDtypeStruct((8, OWN), F32)],
        in_specs=[vm, vm, vm, hbm],
        out_specs=[hbm, vm],
        scratch_shapes=[
            pltpu.VMEM((2, 8, OWN, COLS), F32), pltpu.VMEM((8, OWN, d), BF16), pltpu.VMEM((d, 256), BF16), pltpu.VMEM((d, 768), BF16),
            pltpu.VMEM((SLOTS, TILE, d), BF16), pltpu.VMEM((SUB, 768), F32), pltpu.VMEM((SUB, 768), F32),
            pltpu.VMEM((8, 8 * OWN), jnp.int32), pltpu.VMEM((8, 8 * OWN), F32), pltpu.VMEM((8, 8 * OWN), F32),
            pltpu.VMEM((8, 2, OWN), F32), pltpu.VMEM((8, 8, 2, OWN), F32),
            pltpu.SemaphoreType.DMA((SLOTS,)), pltpu.SemaphoreType.DMA((8,)),
            pltpu.SemaphoreType.DMA((2, 4)), pltpu.SemaphoreType.DMA((2, 2)), pltpu.SemaphoreType.DMA((2, 4)), pltpu.SemaphoreType.DMA((2, 7))],
        compiler_params=pltpu.CompilerParams(collective_id=1, has_side_effects=True, vmem_limit_bytes=VMEM_MAX),
        name='head',
    )(y_own, gains, tgt, table)


def solution(mesh):
    in_specs = (P(), P(), P(), P(), P(None, 't'), P(None, 't'), P(None, 't'), P('t', None), P(), P(), P(None, 't'), P(None, 't'), P('t', None), P(), P(), P(None, None, 't', None), P(None, None, 't', None), P(('v', 't'), None))

    def local_step(hidden_in, seq_lens, target, g_attn_pre, w_q, w_k, w_v, w_o, g_attn_post, g_mlp_pre, w_gate, w_up, w_down, g_mlp_post, g_final, k_cache, v_cache, embed_table):
        picks = lax.broadcasted_iota(jnp.int32, (5, hidden_in.shape[1]), 0)
        gains = g_final[None]
        for i, g in enumerate((g_attn_pre, g_attn_post, g_mlp_pre, g_mlp_post)):
            gains = jnp.where(picks == i, g[None], gains)
        gains = gains.astype(F32)
        freq = jnp.asarray((ROPE_BASE ** (-2.0 * np.arange(128, dtype=np.float32) / 256)).astype(np.float32)[None])
        y_own = layer(hidden_in, seq_lens.reshape(8, 1, OWN), gains, freq, w_q, w_k, w_v, w_o,
                      k_cache.reshape(-1, 256), v_cache.reshape(-1, 256), w_gate, w_up, w_down)
        hidden_out, logprob = head(y_own, gains, target.reshape(8, 1, OWN), embed_table)
        return logprob.reshape(-1), hidden_out

    return jax.shard_map(local_step, mesh=mesh, in_specs=in_specs, out_specs=(P(), P()), check_vma=False)
```

time: 336 us -> 318 us (0.946)
  Pallas kernels: 325 us -> 310 us
  local copies, waits for them, and re-layouts: 9.67 us -> 6.09 us
    pallas_call x1 -> x0, Pallas kernels: 15.6 us -> none  [attention(): pl.pallas_call(attn_kernel, grid_spec=pltpu.PrefetchScalarGridSpec(num_sc...]
    pallas_call x1, Pallas kernels: 128 us -> 132 us  [layer(): pl.pallas_call(layer_kernel, out_shape=jax.ShapeDtypeStruct((2, OWN, COLS...]
    pallas_call x1, Pallas kernels: 181 us -> 178 us  [head(): pl.pallas_call(head_kernel, out_shape=[jax.ShapeDtypeStruct((8 * OWN, d),...]
    another operation x6 -> x0, local copies, waits for them, and re-layouts: 3.57 us -> none  [local_step(): jnp.stack([g_attn_pre, g_attn_post, g_mlp_pre, g_mlp_post, g_final])]
where the time goes in v2:
time: 318 us
  Pallas kernels  310 us (97%)
  local copies, waits for them, and re-layouts  6.09 us (2%)
    pallas_call x1, Pallas kernels, head(): pl.pallas_call(head_kernel, out_shape=[jax.ShapeDtypeStruct((8 * OWN, d),...  178 us
    pallas_call x1, Pallas kernels, layer(): pl.pallas_call(layer_kernel, out_shape=jax.ShapeDtypeStruct((2, OWN, COLS...  132 us

profile of v2, /device:TPU:0, one launch (start us, length us, event | category | flops | bytes accessed | tf_op | source)
XLA Modules:
  0.0 318.1 jit_solution(13222757802891749364)
XLA Ops:
  0.7 1.5 select_convert_fusion.gains
  2.1 132.2 %layer.1.y_own = f32[2,128,1152]{2,1,0:T(8,128)} custom-call(bf16[1024,2304]{1,0:T(8,128)(2,1)} %x_hbm.1, s32[8,1,128]{2,1,0:T(1,128)} %bitcast.8, f32[5,2304]{1,0:T(8,128)} %select_convert_fusion.gains, f32[1,128]{1,0:T(1,128)} %constant.10.clone.freq, bf16[2304,512]{1,0:T(8,128)(2,1)} %wq_hbm.1, bf16[2304,256]{1,0:T(8,128)(2,1)} %wk_hbm.1, ...), custom_call_target="tpu_custom_call" | custom-call | tf_op jit(solution)/shard_map/layer/pallas_call | solution.py:278
  134.3 177.7 %head.1 = (bf16[1024,2304]{1,0:T(8,128)(2,1)}, f32[8,128]{1,0:T(8,128)}) custom-call(f32[2,128,1152]{2,1,0:T(8,128)} %layer.1.y_own, f32[5,2304]{1,0:T(8,128)} %select_convert_fusion.gains, s32[8,1,128]{2,1,0:T(1,128)} %bitcast.7, bf16[32000,2304]{1,0:T(8,128)(2,1)} %e_hbm.1), custom_call_target="tpu_custom_call" | custom-call | tf_op jit(solution)/shard_map/head/pallas_call | solution.py:448
  312.0 1.3 copy.23
  313.3 4.8 %copy.24 = bf16[1024,2304]{1,0:T(8,128)(2,1)} copy(bf16[1024,2304]{1,0:T(8,128)(2,1)} %get-tuple-element.13) | data formatting | bytes 9437184
  (2 shorter events, 0.0 us)

commit v3 on v2

--- a/solution.py
+++ b/solution.py
@@ -101,11 +101,26 @@
     return h0 * inv * (1.0 + g_ref[:, :COLS]), h1 * inv * (1.0 + g_ref[:, COLS:])
 
 
-def layer_kernel(x_hbm, lens, gains, freq, wq_hbm, wk_hbm, wv_hbm, wo_hbm, kc_hbm, vc_hbm, wg_hbm, wu_hbm, wd_hbm, y_ref,
-                 bank, xh, x1, p1, r1, r2, r3, r4, fwd, ag, p2, mb, act, lens_s, loads, caches, s1, s2, s3, s4, s5, s6):
+TILE = 1280
+SUB = 320
+SLOTS = 4
+
+
+def head_epilogue(logits, diff, base):
+    tv, n = logits.shape
+    th = jnp.tanh(logits * (1.0 / FINAL_CAP)).reshape(tv // 8, 8, n)
+    ex = jnp.exp2(th * (FINAL_CAP * LOG2E))
+    rows = lax.broadcasted_iota(jnp.int32, th.shape, 0) * 8
+    hit = jnp.where((diff - base)[None] == rows, th, 0.0)
+    return jnp.sum(ex, axis=0), jnp.sum(hit, axis=0)
+
+
+def step_kernel(x_hbm, lens, gains, freq, tgt, wq_hbm, wk_hbm, wv_hbm, wo_hbm, kc_hbm, vc_hbm, wg_hbm, wu_hbm, wd_hbm, e_hbm, y_out, lp_ref,
+                bank, xh, x1, p1, r1, r2, fwd, ag, p2, mb, act, lens_s, ht0, ht1, lg_a, lg_b, dif, tot, hit, sums, fin,
+                loads, caches, e_sem, y_sem, s1, s2, s3, s4, s5, s6, s7, s8, s9, s10, s11, free_sem):
     t, v, tx, ty, tz = place()
     dev_x, dev_y = (tx, v), (ty, v)
-    g_post, g_pre, g_mlp = gains[1:2, :], gains[2:3, :], gains[3:4, :]
+    g_post, g_pre, g_mlp, g_fin = gains[1:2, :], gains[2:3, :], gains[3:4, :], gains[4:5, :]
     d = xh.shape[1]
     rows = lambda q, c: pl.ds(pl.multiple_of(q * OWN + c * PART, PART), PART)
     part = lambda c: pl.ds(pl.multiple_of(c * PART, PART), PART)
@@ -167,12 +182,12 @@
             cp.wait_send()
         return out
 
-    def ag_first(c):
-        return [send(ag.at[h, rows(t, c)], ag.at[h, rows(t, c)], s3, (c, i), dev)
+    def ag_first(c, sems):
+        return [send(ag.at[h, rows(t, c)], ag.at[h, rows(t, c)], sems, (c, i), dev)
                 for i, (h, dev) in enumerate(((0, dev_x), (1, dev_y), (1, dev_x), (0, dev_y)))]
 
-    def ag_second(c):
-        return [send(ag.at[h, rows(q, c)], ag.at[h, rows(q, c)], s4, (c, h), dev) for h, q, dev in ((0, tx, dev_y), (1, ty, dev_x))]
+    def ag_second(c, sems):
+        return [send(ag.at[h, rows(q, c)], ag.at[h, rows(q, c)], sems, (c, h), dev) for h, q, dev in ((0, tx, dev_y), (1, ty, dev_x))]
 
     def each(body):
         lax.fori_loop(0, CHUNKS, lambda c, _: (body(c), 0)[1], 0)
@@ -218,22 +233,25 @@
         m_a, m_b = norm_halves(x_a.astype(F32), x_b.astype(F32), g_pre)
         ag[0, rows(t, c)] = m_a.astype(BF16).astype(F32)
         ag[1, rows(t, c)] = m_b.astype(BF16).astype(F32)
-        for cp in ag_first(c):
+        for cp in ag_first(c, s3):
             cp.start()
 
     @each
     def _(c):
-        for cp, nxt in zip(ag_first(c)[:2], ag_second(c)):
+        for cp, nxt in zip(ag_first(c, s3)[:2], ag_second(c, s4)):
             cp.wait_recv()
             nxt.start()
 
+    pl.semaphore_signal(free_sem, inc=1, device_id=(t, 1 - v), device_id_type=MESH)
     for w in weights:
         w.wait()
 
     @each
     def _(c):
-        for cp in ag_first(c)[2:] + ag_second(c):
+        for cp in ag_first(c, s3)[2:] + ag_second(c, s4):
             cp.wait_recv()
+        for cp in ag_first(c, s3) + ag_second(c, s4):
+            cp.wait_send()
         for q in range(4):
             for h in range(2):
                 mb[PART * q:PART * q + PART, COLS * h:COLS * h + COLS] = ag[h, rows(q, c)].astype(BF16)
@@ -254,106 +272,72 @@
                 return 0
 
             lax.fori_loop(0, COLS // 384, down, 0)
-        for cp in rs_first(p2, r3, s5, c):
+        for cp in rs_first(p2, r1, s5, c):
             cp.start()
 
-    @each
-    def _(c):
-        rs_forward(p2, r3, r4, s5, s6, c)
-
-    @each
-    def _(c):
-        s_a, s_b = norm_halves(*rs_finish(p2, r3, r4, s5, s6, c), g_mlp)
-        y_ref[0, part(c)] = (x1[part(c), :COLS].astype(F32) + s_a).astype(BF16).astype(F32)
-        y_ref[1, part(c)] = (x1[part(c), COLS:].astype(F32) + s_b).astype(BF16).astype(F32)
-        for cp in ag_first(c) + ag_second(c):
-            cp.wait_send()
-
-
-def layer(x, lens, gains, freq, wq, wk, wv, wo, kc, vc, wg, wu, wd):
-    d = x.shape[1]
-    n = x.shape[0] // 2
-    vm, hbm = pl.BlockSpec(memory_space=pltpu.VMEM), pl.BlockSpec(memory_space=pl.ANY)
-    sem = lambda k: pltpu.SemaphoreType.DMA((2, CHUNKS, k))
-    return pl.pallas_call(
-        layer_kernel,
-        out_shape=jax.ShapeDtypeStruct((2, OWN, COLS), F32),
-        in_specs=[hbm, vm, vm, vm] + [hbm] * 9,
-        out_specs=vm,
-        scratch_shapes=[
-            pltpu.VMEM((3 * d, d), BF16), pltpu.VMEM((n, d), BF16), pltpu.VMEM((OWN, d), BF16), pltpu.VMEM((2, n, COLS), F32),
-            pltpu.VMEM((2, 2, OWN, COLS), F32), pltpu.VMEM((2, OWN, COLS), F32),
-            pltpu.VMEM((2, 2, OWN, COLS), F32), pltpu.VMEM((2, OWN, COLS), F32),
-            pltpu.VMEM((2, OWN, COLS), F32), pltpu.VMEM((2, n, COLS), F32), pltpu.VMEM((2, n, COLS), F32),
-            pltpu.VMEM((OWN, d), BF16), pltpu.VMEM((OWN, d), BF16), pltpu.VMEM((n, 128), jnp.int32),
-            pltpu.SemaphoreType.DMA((8,)), pltpu.SemaphoreType.DMA((CHUNKS, 8)),
-            sem(4), sem(2), sem(4), sem(2), sem(4), sem(2)],
-        compiler_params=pltpu.CompilerParams(collective_id=0, has_side_effects=True, vmem_limit_bytes=VMEM_MAX),
-        name='layer',
-    )(x, lens, gains, freq, wq, wk, wv, wo, kc, vc, wg, wu, wd)
-
-
-TILE = 1280
-SUB = 320
-SLOTS = 3
-
-
-def head_epilogue(logits, diff, base):
-    tv, n = logits.shape
-    th = jnp.tanh(logits * (1.0 / FINAL_CAP)).reshape(tv // 8, 8, n)
-    ex = jnp.exp2(th * (FINAL_CAP * LOG2E))
-    rows = lax.broadcasted_iota(jnp.int32, th.shape, 0) * 8
-    hit = jnp.where((diff - base)[None] == rows, th, 0.0)
-    return jnp.sum(ex, axis=0), jnp.sum(hit, axis=0)
-
-
-def head_kernel(y_own, gains, tgt, e_hbm, y_out, lp_ref,
-                ag, yb, ht0, ht1, eb, lg_a, lg_b, dif, tot, hit, part, fin, e_sem, y_sem, s1, s2, s3, s4):
-    t, v, tx, ty, tz = place()
-    me = v * 4 + t
-    dev_x, dev_y, dev_p = (tx, v), (ty, v), (t, 1 - v)
-    g_fin = gains[4:5, :]
+    me, oth = v * 4 + t, p1
+    eb = bank.at[:SLOTS * TILE]
+    yb = bank.at[SLOTS * TILE:SLOTS * TILE + 8 * OWN]
     tiles = e_hbm.shape[0] // TILE
     total = 2 * tiles
 
+    def slot_of(g):
+        return pl.ds(pl.multiple_of((g % SLOTS) * TILE, TILE), TILE)
+
     def fetch(g):
         src = e_hbm.at[pl.ds(pl.multiple_of((g % tiles) * TILE, TILE), TILE)]
-        return pltpu.make_async_copy(src, eb.at[g % SLOTS], e_sem.at[g % SLOTS])
-
-    for g in range(SLOTS - 1):
+        return local(src, eb.at[slot_of(g)], e_sem.at[g % SLOTS])
+
+    for g in range(SLOTS):
         fetch(g).start()
-    meet_all(t, v)
-
-    first = [send(y_own.at[h], ag.at[h, me], s1, (i,), dev)
-             for i, (h, dev) in enumerate(((0, dev_x), (1, dev_y), (1, dev_x), (0, dev_y)))]
-    second = [send(ag.at[h, v * 4 + q], ag.at[h, v * 4 + q], s2, (h,), dev) for h, q, dev in ((0, tx, dev_y), (1, ty, dev_x))]
-    cross = [send(y_own, ag.at[:, me], s3, (0,), dev_p)]
-    cross += [send(ag.at[:, v * 4 + q], ag.at[:, v * 4 + q], s3, (i + 1,), dev_p) for i, q in enumerate((tx, ty, tz))]
-    cross[0].start()
-    for cp in first:
-        cp.start()
+
+    @each
+    def _(c):
+        rs_forward(p2, r1, r2, s5, s6, c)
+
+    def cross_own(c):
+        return send(ag.at[:, rows(t, c)], oth.at[:, rows(t, c)], s9, (c,), (t, 1 - v))
+
+    pl.semaphore_wait(free_sem, 1)
+
+    @each
+    def _(c):
+        s_a, s_b = norm_halves(*rs_finish(p2, r1, r2, s5, s6, c), g_mlp)
+        ag[0, rows(t, c)] = (x1[part(c), :COLS].astype(F32) + s_a).astype(BF16).astype(F32)
+        ag[1, rows(t, c)] = (x1[part(c), COLS:].astype(F32) + s_b).astype(BF16).astype(F32)
+        cross_own(c).start()
+        for cp in ag_first(c, s7):
+            cp.start()
+
+    block = lambda q: pl.ds(pl.multiple_of(q * OWN, OWN), OWN)
+    cross = [send(ag.at[:, block(q)], oth.at[:, block(q)], s10, (i,), (t, 1 - v)) for i, q in enumerate((tx, ty, tz))]
     tot[...] = jnp.zeros_like(tot)
     hit[...] = jnp.zeros_like(hit)
-    spots = [w * 4 + q for q in (t, tx, ty, tz) for w in range(2)]
+    spots = [w * 4 + q for q in (t, tx, ty, tz) for w in (v, 1 - v)]
     for k, b in enumerate(spots):
         lane = tgt[b] - me * e_hbm.shape[0]
         dif[:, OWN * k:OWN * k + OWN] = lane - lax.broadcasted_iota(jnp.int32, (8, OWN), 0)
 
     def y_copy(b):
-        return pltpu.make_async_copy(yb.at[b], y_out.at[pl.ds(pl.multiple_of(b * OWN, OWN), OWN)], y_sem.at[b])
-
-    def prepare(h_a, h_b, b, ht, lanes):
-        yb[b, :, :COLS] = h_a.astype(BF16)
-        yb[b, :, COLS:] = h_b.astype(BF16)
+        return local(yb.at[block(b)], y_out.at[block(b)], y_sem.at[b])
+
+    def prepare(src, w, q, ht, lanes):
+        h_a, h_b = src[0, block(q)], src[1, block(q)]
+        b = w * 4 + q
+        yb[block(b), :COLS] = h_a.astype(BF16)
+        yb[block(b), COLS:] = h_b.astype(BF16)
         y_copy(b).start()
         n_a, n_b = norm_halves(h_a, h_b, g_fin)
         ht[:COLS, lanes] = n_a.T.astype(BF16)
         ht[COLS:, lanes] = n_b.T.astype(BF16)
 
-    cross[0].wait_recv()
-    other = (1 - v) * 4 + t
-    prepare(y_own[0], y_own[1], me, ht0, pl.ds(pl.multiple_of(v * OWN, OWN), OWN))
-    prepare(ag[0, other], ag[1, other], other, ht0, pl.ds(pl.multiple_of((1 - v) * OWN, OWN), OWN))
+    prepare(ag, v, t, ht0, slice(0, OWN))
+
+    @each
+    def _(c):
+        cross_own(c).wait_recv()
+
+    prepare(oth, 1 - v, t, ht0, slice(OWN, 2 * OWN))
 
     def epilogue(lg, span, base, valid):
         s, k = head_epilogue(lg, dif[:, span], base)
@@ -362,104 +346,146 @@
 
     def body(i, offset, ht, bufs, span):
         g = i + offset
-        slot = g % SLOTS
         fetch(g).wait()
 
-        @pl.when(g + SLOTS - 1 < total)
+        @pl.when((g >= 1) & (g + SLOTS - 1 < total))
         def _():
             fetch(g + SLOTS - 1).start()
 
+        first = pl.multiple_of((g % SLOTS) * TILE, TILE)
         for k in range(TILE // SUB):
             cur, prev = bufs[k % 2], bufs[(k + 1) % 2]
-            cur[...] = jnp.dot(eb[slot, SUB * k:SUB * k + SUB, :], ht[...], preferred_element_type=F32)
+            cur[...] = jnp.dot(bank[pl.ds(first + SUB * k, SUB), :], ht[...], preferred_element_type=F32)
             epilogue(prev[...], span, i * TILE + (k - 1) * SUB, True if k else i > 0)
 
     near, far = slice(0, 2 * OWN), slice(2 * OWN, 8 * OWN)
     near_bufs = (lg_a.at[:, near], lg_b.at[:, near])
 
     def pass_one(i, _):
-        @pl.when(i == 9)
-        def _():
-            for cp, nxt in zip(first[:2], second):
+        @pl.when((i >= 3) & (i < 15) & (i % 3 == 0))
+        def _():
+            c = i // 3 - 1
+            for cp, nxt in zip(ag_first(c, s7)[:2], ag_second(c, s8)):
                 cp.wait_recv()
                 nxt.start()
 
-        @pl.when(i == 15)
-        def _():
-            for cp in first[2:]:
-                cp.wait_recv()
+        @pl.when(i == 16)
+        def _():
+            for c in range(CHUNKS):
+                for cp in ag_first(c, s7)[2:]:
+                    cp.wait_recv()
+            cross[0].start()
             cross[1].start()
+
+        @pl.when((i == 18) | (i == 20))
+        def _():
+            k = i - 18
+            prepare(ag, v, tx + (k // 2) * (ty - tx), ht1, pl.ds(pl.multiple_of(k * OWN, OWN), OWN))
+
+        @pl.when(i == 19)
+        def _():
+            cross[0].wait_recv()
+            cross[1].wait_recv()
+
+        @pl.when((i == 19) | (i == 21))
+        def _():
+            k = i - 18
+            prepare(oth, 1 - v, tx + (k // 2) * (ty - tx), ht1, pl.ds(pl.multiple_of(k * OWN, OWN), OWN))
+
+        @pl.when(i == 23)
+        def _():
+            for c in range(CHUNKS):
+                for cp in ag_second(c, s8):
+                    cp.wait_recv()
             cross[2].start()
-
-        @pl.when(i == 17)
-        def _():
-            cross[1].wait_recv()
-            cross[2].wait_recv()
-
-        @pl.when((i >= 17) & (i < 21))
-        def _():
-            k = i - 17
-            chip = tx + (k // 2) * (ty - tx)
-            b = (k % 2) * 4 + chip
-            prepare(ag[0, b], ag[1, b], b, ht1, pl.ds(pl.multiple_of(k * OWN, OWN), OWN))
-
-        @pl.when(i == 23)
-        def _():
-            for cp in second:
-                cp.wait_recv()
-            cross[3].start()
 
         body(i, 0, ht0, near_bufs, near)
         return 0
 
     lax.fori_loop(0, tiles, pass_one, 0)
     epilogue(lg_b[:, near], near, tiles * TILE - SUB, True)
-    cross[3].wait_recv()
-    for k in (4, 5):
-        b = (k % 2) * 4 + tz
-        prepare(ag[0, b], ag[1, b], b, ht1, slice(OWN * k, OWN * k + OWN))
+    prepare(ag, v, tz, ht1, slice(4 * OWN, 5 * OWN))
+    cross[2].wait_recv()
+    prepare(oth, 1 - v, tz, ht1, slice(5 * OWN, 6 * OWN))
     lax.fori_loop(0, tiles, lambda i, _: (body(i, tiles, ht1, (lg_a, lg_b), far), 0)[1], 0)
     epilogue(lg_b[...], far, tiles * TILE - SUB, True)
 
     for k, b in enumerate(spots):
         lanes = slice(OWN * k, OWN * k + OWN)
-        part[b, 0:1] = jnp.sum(tot[:, lanes], axis=0, keepdims=True)
-        part[b, 1:2] = jnp.sum(hit[:, lanes], axis=0, keepdims=True)
+        sums[b, 0:1] = jnp.sum(tot[:, lanes], axis=0, keepdims=True)
+        sums[b, 1:2] = jnp.sum(hit[:, lanes], axis=0, keepdims=True)
     outs = []
     for k in range(1, 8):
         dt, dv = k % 4, k // 4
-        outs.append(send(part, fin.at[k], s4, (k - 1,), ((t + dt) % 4, (v + dv) % 2)))
+        outs.append(send(sums, fin.at[k], s11, (k - 1,), ((t + dt) % 4, (v + dv) % 2)))
     for cp in outs:
         cp.start()
-    acc = part[...]
+    acc = sums[...]
     for k in range(1, 8):
         outs[k - 1].wait_recv()
         acc += fin[k]
     lp_ref[...] = FINAL_CAP * acc[:, 1] - jnp.log(acc[:, 0])
-    for cp in first + second + cross + outs:
+    for c in range(CHUNKS):
+        for cp in ag_first(c, s7) + ag_second(c, s8) + [cross_own(c)]:
+            cp.wait_send()
+    for cp in cross + outs:
         cp.wait_send()
     for b in range(8):
         y_copy(b).wait()
 
 
-def head(y_own, gains, tgt, table):
-    d = table.shape[1]
+def step(x, lens, gains, freq, tgt, wq, wk, wv, wo, kc, vc, wg, wu, wd, table):
+    d = x.shape[1]
+    n = x.shape[0] // 2
+    vm, hbm = pl.BlockSpec(memory_space=pltpu.VMEM), pl.BlockSpec(memory_space=pl.ANY)
+    sem = lambda *k: pltpu.SemaphoreType.DMA(k)
+    return pl.pallas_call(
+        step_kernel,
+        out_shape=[jax.ShapeDtypeStruct(x.shape, BF16), jax.ShapeDtypeStruct((8, OWN), F32)],
+        in_specs=[hbm, vm, vm, vm, vm] + [hbm] * 10,
+        out_specs=[hbm, vm],
+        scratch_shapes=[
+            pltpu.VMEM((3 * d, d), BF16), pltpu.VMEM((n, d), BF16), pltpu.VMEM((OWN, d), BF16), pltpu.VMEM((2, n, COLS), F32),
+            pltpu.VMEM((2, 2, OWN, COLS), F32), pltpu.VMEM((2, OWN, COLS), F32),
+            pltpu.VMEM((2, OWN, COLS), F32), pltpu.VMEM((2, n, COLS), F32), pltpu.VMEM((2, n, COLS), F32),
+            pltpu.VMEM((OWN, d), BF16), pltpu.VMEM((OWN, d), BF16), pltpu.VMEM((n, 128), jnp.int32),
+            pltpu.VMEM((d, 256), BF16), pltpu.VMEM((d, 768), BF16), pltpu.VMEM((SUB, 768), F32), pltpu.VMEM((SUB, 768), F32),
+            pltpu.VMEM((8, 8 * OWN), jnp.int32), pltpu.VMEM((8, 8 * OWN), F32), pltpu.VMEM((8, 8 * OWN), F32),
+            pltpu.VMEM((8, 2, OWN), F32), pltpu.VMEM((8, 8, 2, OWN), F32),
+            sem(8), sem(CHUNKS, 8), sem(SLOTS), sem(8),
+            sem(2, CHUNKS, 4), sem(2, CHUNKS, 2), sem(2, CHUNKS, 4), sem(2, CHUNKS, 2), sem(2, CHUNKS, 4), sem(2, CHUNKS, 2),
+            sem(2, CHUNKS, 4), sem(2, CHUNKS, 2), sem(2, CHUNKS), sem(2, 3), sem(2, 7), pltpu.SemaphoreType.REGULAR],
+        compiler_params=pltpu.CompilerParams(collective_id=0, has_side_effects=True, vmem_limit_bytes=VMEM_MAX),
+        name='step',
+    )(x, lens, gains, freq, tgt, wq, wk, wv, wo, kc, vc, wg, wu, wd, table)
+
+
+def finish_kernel(y_hbm, lp_ref, y_out, lp_out, yb, sems):
+    blocks = yb.shape[0]
+    rows = yb.shape[1]
+    take = [pltpu.make_async_copy(y_hbm.at[rows * i:rows * i + rows], yb.at[i], sems.at[0, i]) for i in range(blocks)]
+    give = [pltpu.make_async_copy(yb.at[i], y_out.at[rows * i:rows * i + rows], sems.at[1, i]) for i in range(blocks)]
+    for cp in take:
+        cp.start()
+    lp_out[...] = lp_ref[...]
+    for a, b in zip(take, give):
+        a.wait()
+        b.start()
+    for cp in give:
+        cp.wait()
+
+
+def finish(y, lp):
     vm, hbm = pl.BlockSpec(memory_space=pltpu.VMEM), pl.BlockSpec(memory_space=pl.ANY)
     return pl.pallas_call(
-        head_kernel,
-        out_shape=[jax.ShapeDtypeStruct((8 * OWN, d), BF16), jax.ShapeDtypeStruct((8, OWN), F32)],
-        in_specs=[vm, vm, vm, hbm],
+        finish_kernel,
+        out_shape=[jax.ShapeDtypeStruct(y.shape, y.dtype), jax.ShapeDtypeStruct(lp.shape, lp.dtype)],
+        in_specs=[hbm, vm],
         out_specs=[hbm, vm],
-        scratch_shapes=[
-            pltpu.VMEM((2, 8, OWN, COLS), F32), pltpu.VMEM((8, OWN, d), BF16), pltpu.VMEM((d, 256), BF16), pltpu.VMEM((d, 768), BF16),
-            pltpu.VMEM((SLOTS, TILE, d), BF16), pltpu.VMEM((SUB, 768), F32), pltpu.VMEM((SUB, 768), F32),
-            pltpu.VMEM((8, 8 * OWN), jnp.int32), pltpu.VMEM((8, 8 * OWN), F32), pltpu.VMEM((8, 8 * OWN), F32),
-            pltpu.VMEM((8, 2, OWN), F32), pltpu.VMEM((8, 8, 2, OWN), F32),
-            pltpu.SemaphoreType.DMA((SLOTS,)), pltpu.SemaphoreType.DMA((8,)),
-            pltpu.SemaphoreType.DMA((2, 4)), pltpu.SemaphoreType.DMA((2, 2)), pltpu.SemaphoreType.DMA((2, 4)), pltpu.SemaphoreType.DMA((2, 7))],
-        compiler_params=pltpu.CompilerParams(collective_id=1, has_side_effects=True, vmem_limit_bytes=VMEM_MAX),
-        name='head',
-    )(y_own, gains, tgt, table)
+        scratch_shapes=[pltpu.VMEM((8, y.shape[0] // 8, y.shape[1]), y.dtype), pltpu.SemaphoreType.DMA((2, 8))],
+        compiler_params=pltpu.CompilerParams(vmem_limit_bytes=VMEM_LIMIT),
+        name='finish',
+    )(y, lp)
 
 
 def solution(mesh):
@@ -472,9 +498,9 @@
             gains = jnp.where(picks == i, g[None], gains)
         gains = gains.astype(F32)
         freq = jnp.asarray((ROPE_BASE ** (-2.0 * np.arange(128, dtype=np.float32) / 256)).astype(np.float32)[None])
-        y_own = layer(hidden_in, seq_lens.reshape(8, 1, OWN), gains, freq, w_q, w_k, w_v, w_o,
-                      k_cache.reshape(-1, 256), v_cache.reshape(-1, 256), w_gate, w_up, w_down)
-        hidden_out, logprob = head(y_own, gains, target.reshape(8, 1, OWN), embed_table)
+        hidden_out, logprob = step(hidden_in, seq_lens.reshape(8, 1, OWN), gains, freq, target.reshape(8, 1, OWN), w_q, w_k, w_v, w_o,
+                      k_cache.reshape(-1, 256), v_cache.reshape(-1, 256), w_gate, w_up, w_down, embed_table)
+        hidden_out, logprob = finish(hidden_out, logprob)
         return logprob.reshape(-1), hidden_out
 
     return jax.shard_map(local_step, mesh=mesh, in_specs=in_specs, out_specs=(P(), P()), check_vma=False)

time: 318 us -> 315 us (level)
  local copies, waits for them, and re-layouts: 6.09 us -> 0 us
    unnamed x2 -> x0, local copies, waits for them, and re-layouts: 6.09 us -> none
where the time goes in v3:
time: 315 us; the launch traced here: 314 us
  Pallas kernels  312 us (99%)
    pallas_call x1, Pallas kernels, step(): pl.pallas_call(step_kernel, out_shape=[jax.ShapeDtypeStruct(x.shape, BF16...  307 us

profile of v3, /device:TPU:0, one launch (start us, length us, event | category | flops | bytes accessed | tf_op | source)
XLA Modules:
  0.0 314.4 jit_solution(6152848701264231515)
XLA Ops:
  0.7 1.5 select_convert_fusion.gains
  2.1 306.9 %step.1 = (bf16[1024,2304]{1,0:T(8,128)(2,1)}, f32[8,128]{1,0:T(8,128)}) custom-call(bf16[1024,2304]{1,0:T(8,128)(2,1)} %x_hbm.1, s32[8,1,128]{2,1,0:T(1,128)} %bitcast.7, f32[5,2304]{1,0:T(8,128)} %select_convert_fusion.gains, f32[1,128]{1,0:T(1,128)} %constant.10.clone.freq, s32[8,1,128]{2,1,0:T(1,128)} %bitcast.8, bf16[2304,512]{1,0:T(8,128)(2,1)} %wq_hbm.1, ...), custom_call_target="tpu_custom_call" | custom-call | tf_op jit(solution)/shard_map/step/pallas_call | solution.py:442
  309.0 5.4 %finish.1 = (bf16[1024,2304]{1,0:T(8,128)(2,1)}, f32[8,128]{1,0:T(8,128)}) custom-call(bf16[1024,2304]{1,0:T(8,128)(2,1)} %get-tuple-element.6.y_hbm, f32[8,128]{1,0:T(8,128)} %get-tuple-element.7.lp_ref), custom_call_target="tpu_custom_call" | custom-call | tf_op jit(solution)/shard_map/finish/pallas_call | solution.py:480
  (2 shorter events, 0.0 us)

commit v4 on v3

--- a/solution.py
+++ b/solution.py
@@ -115,11 +115,13 @@
     return jnp.sum(ex, axis=0), jnp.sum(hit, axis=0)
 
 
-def step_kernel(x_hbm, lens, gains, freq, tgt, wq_hbm, wk_hbm, wv_hbm, wo_hbm, kc_hbm, vc_hbm, wg_hbm, wu_hbm, wd_hbm, e_hbm, y_out, lp_ref,
-                bank, xh, x1, p1, r1, r2, fwd, ag, p2, mb, act, lens_s, ht0, ht1, lg_a, lg_b, dif, tot, hit, sums, fin,
+def step_kernel(x_hbm, lens, ga, gb, gc, gd, ge, freq, tgt, wq_hbm, wk_hbm, wv_hbm, wo_hbm, kc_hbm, vc_hbm, wg_hbm, wu_hbm, wd_hbm, e_hbm, y_out, lp_ref,
+                bank, xh, x1, p1, r1, r2, fwd, ag, p2, mb, act, gains, lens_s, ht0, ht1, lg_a, lg_b, dif, tot, hit, sums, fin,
                 loads, caches, e_sem, y_sem, s1, s2, s3, s4, s5, s6, s7, s8, s9, s10, s11, free_sem):
     t, v, tx, ty, tz = place()
     dev_x, dev_y = (tx, v), (ty, v)
+    for i, g in enumerate((ga, gb, gc, gd, ge)):
+        gains[i:i + 1, :] = g[...].astype(F32).reshape(1, -1)
     g_post, g_pre, g_mlp, g_fin = gains[1:2, :], gains[2:3, :], gains[3:4, :], gains[4:5, :]
     d = xh.shape[1]
     rows = lambda q, c: pl.ds(pl.multiple_of(q * OWN + c * PART, PART), PART)
@@ -328,8 +330,8 @@
         yb[block(b), COLS:] = h_b.astype(BF16)
         y_copy(b).start()
         n_a, n_b = norm_halves(h_a, h_b, g_fin)
-        ht[:COLS, lanes] = n_a.T.astype(BF16)
-        ht[COLS:, lanes] = n_b.T.astype(BF16)
+        ht[:COLS, lanes] = n_a.astype(BF16).T
+        ht[COLS:, lanes] = n_b.astype(BF16).T
 
     prepare(ag, v, t, ht0, slice(0, OWN))
 
@@ -434,7 +436,7 @@
         y_copy(b).wait()
 
 
-def step(x, lens, gains, freq, tgt, wq, wk, wv, wo, kc, vc, wg, wu, wd, table):
+def step(x, lens, ga, gb, gc, gd, ge, freq, tgt, wq, wk, wv, wo, kc, vc, wg, wu, wd, table):
     d = x.shape[1]
     n = x.shape[0] // 2
     vm, hbm = pl.BlockSpec(memory_space=pltpu.VMEM), pl.BlockSpec(memory_space=pl.ANY)
@@ -442,13 +444,13 @@
     return pl.pallas_call(
         step_kernel,
         out_shape=[jax.ShapeDtypeStruct(x.shape, BF16), jax.ShapeDtypeStruct((8, OWN), F32)],
-        in_specs=[hbm, vm, vm, vm, vm] + [hbm] * 10,
+        in_specs=[hbm] + [vm] * 8 + [hbm] * 10,
         out_specs=[hbm, vm],
         scratch_shapes=[
             pltpu.VMEM((3 * d, d), BF16), pltpu.VMEM((n, d), BF16), pltpu.VMEM((OWN, d), BF16), pltpu.VMEM((2, n, COLS), F32),
             pltpu.VMEM((2, 2, OWN, COLS), F32), pltpu.VMEM((2, OWN, COLS), F32),
             pltpu.VMEM((2, OWN, COLS), F32), pltpu.VMEM((2, n, COLS), F32), pltpu.VMEM((2, n, COLS), F32),
-            pltpu.VMEM((OWN, d), BF16), pltpu.VMEM((OWN, d), BF16), pltpu.VMEM((n, 128), jnp.int32),
+            pltpu.VMEM((OWN, d), BF16), pltpu.VMEM((OWN, d), BF16), pltpu.VMEM((8, d), F32), pltpu.VMEM((n, 128), jnp.int32),
             pltpu.VMEM((d, 256), BF16), pltpu.VMEM((d, 768), BF16), pltpu.VMEM((SUB, 768), F32), pltpu.VMEM((SUB, 768), F32),
             pltpu.VMEM((8, 8 * OWN), jnp.int32), pltpu.VMEM((8, 8 * OWN), F32), pltpu.VMEM((8, 8 * OWN), F32),
             pltpu.VMEM((8, 2, OWN), F32), pltpu.VMEM((8, 8, 2, OWN), F32),
@@ -457,7 +459,7 @@
             sem(2, CHUNKS, 4), sem(2, CHUNKS, 2), sem(2, CHUNKS), sem(2, 3), sem(2, 7), pltpu.SemaphoreType.REGULAR],
         compiler_params=pltpu.CompilerParams(collective_id=0, has_side_effects=True, vmem_limit_bytes=VMEM_MAX),
         name='step',
-    )(x, lens, gains, freq, tgt, wq, wk, wv, wo, kc, vc, wg, wu, wd, table)
+    )(x, lens, ga, gb, gc, gd, ge, freq, tgt, wq, wk, wv, wo, kc, vc, wg, wu, wd, table)
 
 
 def finish_kernel(y_hbm, lp_ref, y_out, lp_out, yb, sems):
@@ -492,13 +494,8 @@
     in_specs = (P(), P(), P(), P(), P(None, 't'), P(None, 't'), P(None, 't'), P('t', None), P(), P(), P(None, 't'), P(None, 't'), P('t', None), P(), P(), P(None, None, 't', None), P(None, None, 't', None), P(('v', 't'), None))
 
     def local_step(hidden_in, seq_lens, target, g_attn_pre, w_q, w_k, w_v, w_o, g_attn_post, g_mlp_pre, w_gate, w_up, w_down, g_mlp_post, g_final, k_cache, v_cache, embed_table):
-        picks = lax.broadcasted_iota(jnp.int32, (5, hidden_in.shape[1]), 0)
-        gains = g_final[None]
-        for i, g in enumerate((g_attn_pre, g_attn_post, g_mlp_pre, g_mlp_post)):
-            gains = jnp.where(picks == i, g[None], gains)
-        gains = gains.astype(F32)
         freq = jnp.asarray((ROPE_BASE ** (-2.0 * np.arange(128, dtype=np.float32) / 256)).astype(np.float32)[None])
-        hidden_out, logprob = step(hidden_in, seq_lens.reshape(8, 1, OWN), gains, freq, target.reshape(8, 1, OWN), w_q, w_k, w_v, w_o,
+        hidden_out, logprob = step(hidden_in, seq_lens.reshape(8, 1, OWN), g_attn_pre, g_attn_post, g_mlp_pre, g_mlp_post, g_final, freq, target.reshape(8, 1, OWN), w_q, w_k, w_v, w_o,
                       k_cache.reshape(-1, 256), v_cache.reshape(-1, 256), w_gate, w_up, w_down, embed_table)
         hidden_out, logprob = finish(hidden_out, logprob)
         return logprob.reshape(-1), hidden_out

time: 315 us -> 313 us (level)
  no operation moved by 1% of the time
where the time goes in v4:
time: 313 us
  Pallas kernels  312 us (100%)
    pallas_call x1, Pallas kernels, step(): pl.pallas_call(step_kernel, out_shape=[jax.ShapeDtypeStruct(x.shape, BF16...  307 us

profile of v4, /device:TPU:0, one launch (start us, length us, event | category | flops | bytes accessed | tf_op | source)
XLA Modules:
  0.0 313.0 jit_solution(11747550499259005449)
XLA Ops:
  0.6 307.0 %step.1 = (bf16[1024,2304]{1,0:T(8,128)(2,1)}, f32[8,128]{1,0:T(8,128)}) custom-call(bf16[1024,2304]{1,0:T(8,128)(2,1)} %x_hbm.1, s32[8,1,128]{2,1,0:T(1,128)} %bitcast.7, bf16[2304]{0:T(1024)(128)(2,1)} %ga.1, bf16[2304]{0:T(1024)(128)(2,1)} %gb.1, bf16[2304]{0:T(1024)(128)(2,1)} %gc.1, bf16[2304]{0:T(1024)(128)(2,1)} %gd.1, bf16[2304]{0:T(1024)(128)(2,1)} %ge.1, ...), custom_call_target="tpu_custom_call" | custom-call | tf_op jit(solution)/shard_map/step/pallas_call | solution.py:444
  307.6 5.4 %finish.1 = (bf16[1024,2304]{1,0:T(8,128)(2,1)}, f32[8,128]{1,0:T(8,128)}) custom-call(bf16[1024,2304]{1,0:T(8,128)(2,1)} %get-tuple-element.6.y_hbm, f32[8,128]{1,0:T(8,128)} %get-tuple-element.7.lp_ref), custom_call_target="tpu_custom_call" | custom-call | tf_op jit(solution)/shard_map/finish/pallas_call | solution.py:482
